TPU v7x, 128 devices: a whole 4x4x4 slice. The times are simulated.
128 devices in a mesh: node: 8 (over x, core), local: 16 (over y, z).
Axes of the slice: x: 4, y: 4, z: 4, core: 2. Of those that a mesh axis runs over, the one named last changes fastest.
Arguments:
- tokens: bfloat16 [8192, 7168], P(('node', 'local')), may hold values from -6 to 6
- routes: int32 [8192, 2], P(('node', 'local')), may hold values from 0 to 31, as said below
- scores: float32 [8192, 2], P(('node', 'local')), may hold values from 0.1 to 1
- gate_proj: bfloat16 [128, 7168, 512], P(('node', 'local')), may hold values from -0.0625 to 0.0625
- up_proj: bfloat16 [128, 7168, 512], P(('node', 'local')), may hold values from -0.0625 to 0.0625
- down_proj: bfloat16 [128, 512, 7168], P(('node', 'local')), may hold values from -0.125 to 0.125
Outputs:
- combined: bfloat16 [8192, 7168], P(('node', 'local'))
Inputs may be any that keep to these rules, and one draw needn't show every extreme that they name: `routes`: each row names 2 different experts. The rows of one device name each expert at most 5 times, and in every draw one expert is named by exactly 5 rows of every device.
All inputs are finite; a program needn't handle non-finite values.
Results may differ from a plain program's by a relative error of at most 0.0085.
Values may be sent and summed in bfloat16 or wider, within the bound.
No kernel may reach another device: no remote copies, remote signals or barrier semaphores. Data moves between devices by JAX's collectives and lax.ppermute only.
A program may use at most 192 MiB of HBM per device.

v0:
```python
import jax
import jax.numpy as jnp
from jax import lax
from jax.sharding import PartitionSpec as P

SHARDS = 4


SCALE = 2.827


def expert_block(block_rows, w_gate, w_up, w_down):
    block_shape = block_rows.shape
    flat_rows = block_rows.reshape(-1, block_shape[-1])
    gate_act = jnp.dot(flat_rows, w_gate, preferred_element_type=jnp.float32)
    up_act = jnp.dot(flat_rows, w_up, preferred_element_type=jnp.float32)
    hidden = (jax.nn.silu(gate_act) * up_act).astype(jnp.bfloat16)
    partial_value = jnp.dot(hidden, w_down, preferred_element_type=jnp.float32).astype(jnp.bfloat16)
    return partial_value.reshape(block_shape[:-1] + (w_down.shape[1],))


def per_device(tokens, routes, scores, gate_proj, up_proj, down_proj):
    node_count = lax.axis_size("node")
    local_count = lax.axis_size("local")
    token_count, model_width = tokens.shape
    top_count = routes.shape[1]
    node_experts = local_count // SHARDS
    experts = node_count * node_experts
    per_expert = max(
        2, token_count * top_count // experts + token_count * top_count // (4 * experts)
    )
    w_gate = gate_proj[0]
    w_up = up_proj[0]
    w_down = down_proj[0]
    weights = (SCALE * scores / jnp.sum(scores, axis=1, keepdims=True)).astype(jnp.bfloat16)
    labels = jnp.arange(experts, dtype=jnp.int32)
    matches = routes[:, :, None] == labels[None, None, :]
    dense_weight = jnp.sum(jnp.where(matches, weights.astype(jnp.float32)[:, :, None], 0.0), axis=1)
    node_cap = min(token_count, node_experts * per_expert)
    grouped = dense_weight.reshape(token_count, node_count, node_experts)
    reached = jnp.any(grouped > 0, axis=2)
    node_slot = jnp.cumsum(reached.astype(jnp.int32), axis=0) - 1
    slot_index = jnp.arange(node_cap, dtype=jnp.int32)
    node_pick = reached[None] & (node_slot[None] == slot_index[:, None, None])
    send_rows = jnp.einsum(
        "ctn,td->ncd", node_pick.astype(jnp.bfloat16), tokens, preferred_element_type=jnp.float32
    ).astype(jnp.bfloat16)
    send_weight = jnp.einsum(
        "ctn,tnj->ncj", node_pick.astype(jnp.float32), grouped, precision=lax.Precision.HIGHEST
    ).astype(jnp.bfloat16)
    arrived, arrived_weight = (
        lax.all_to_all(send_rows, "node", split_axis=0, concat_axis=0, tiled=True),
        lax.all_to_all(send_weight, "node", split_axis=0, concat_axis=0, tiled=True),
    )
    row_count = node_count * node_cap
    arrived = arrived.reshape(row_count, model_width)
    row_weight = arrived_weight.reshape(row_count, node_experts).astype(jnp.float32)
    capacity = node_count * per_expert
    routed = row_weight > 0
    position = jnp.cumsum(routed.astype(jnp.int32), axis=0) - 1
    slot_ids = jnp.arange(capacity, dtype=jnp.int32)
    slot_pick = (routed[None] & (position[None] == slot_ids[:, None, None])).astype(jnp.bfloat16)
    bucket = jnp.einsum(
        "crj,rd->jcd", slot_pick, arrived, preferred_element_type=jnp.float32
    ).astype(jnp.bfloat16)
    outgoing = jnp.broadcast_to(
        bucket[:, None], (node_experts, SHARDS, capacity, model_width)
    ).reshape(local_count, capacity, model_width)
    results = expert_block(
        lax.all_to_all(outgoing, "local", split_axis=0, concat_axis=0, tiled=True),
        w_gate,
        w_up,
        w_down,
    )
    returned = lax.all_to_all(results, "local", split_axis=0, concat_axis=0, tiled=True)
    summed = jnp.sum(
        returned.reshape(node_experts, SHARDS, capacity, model_width).astype(jnp.float32), axis=1
    )
    local_ids = jnp.arange(node_experts, dtype=jnp.int32)
    gathered = summed[local_ids[None, :], jnp.clip(position, 0, capacity - 1)]
    node_total = jnp.sum(gathered * row_weight[:, :, None], axis=1).reshape(
        node_count, node_cap, model_width
    )
    returned_home = lax.all_to_all(
        node_total.astype(jnp.bfloat16), "node", split_axis=0, concat_axis=0, tiled=True
    ).astype(node_total.dtype)
    node_ids = jnp.arange(node_count, dtype=jnp.int32)
    gathered_home = returned_home[node_ids[None, :], jnp.clip(node_slot, 0, node_cap - 1)]
    combined = jnp.sum(jnp.where(reached[:, :, None], gathered_home, 0.0), axis=1)
    return combined.astype(jnp.bfloat16)


def solution(mesh):
    return jax.shard_map(
        per_device,
        mesh=mesh,
        in_specs=(
            P(("node", "local"), None),
            P(("node", "local"), None),
            P(("node", "local"), None),
            P(("node", "local"), None, None),
            P(("node", "local"), None, None),
            P(("node", "local"), None, None),
        ),
        out_specs=P(("node", "local"), None),
        check_vma=False,
    )
```

profile of v0, /device:TPU:96, one launch (start us, length us, event | category | flops | bytes accessed | tf_op | source)
XLA Modules:
  0.0 517.0 jit_solution(17380416106367744728)
XLA Ops:
  0.0 0.8 reduce_sum.45
  0.8 0.7 fusion.29
  1.5 0.7 select_reduce_fusion
  2.4 0.8 convolution_convert_fusion.3
  3.3 4.3 all-to-all-start.1
  7.6 0.7 fusion.1
  8.3 2.9 copy.70
  11.2 1.7 all-to-all-done.1
  12.9 4.4 all-to-all-start
  17.4 1.2 reduce-window.6
  19.0 0.1 copy.78
  19.3 32.2 %all-to-all-done = bf16[8,20,7168]{2,1,0:T(8,128)(2,1)} async-done(((bf16[8,20,7168]{2,1,0:T(8,128)(2,1)}), bf16[8,20,7168]{2,1,0:T(8,128)(2,1)}, u32[]{:S(2)}, u32[]{:S(2)}) %all-to-all-start) | async-done | bytes 2293792 | tf_op jit(solution)/shard_map/all_to_all | solution.py:52
  51.5 2.7 reshape.113
  54.2 2.1 fusion.2
  56.4 2.9 broadcast_in_dim.31
  59.2 108.7 %all_to_all.25 = bf16[16,40,7168]{2,1,0:T(8,128)(2,1)S(1)} all-to-all(bf16[16,40,7168]{2,1,0:T(8,128)(2,1)S(1)} %bitcast.54), channel_id=1, replica_groups=mesh['node'=8,'local'=16] {'local'}, dimensions={0} | all-to-all | bytes 18350080 | tf_op jit(solution)/shard_map/all_to_all | solution.py:70
  168.0 7.4 %fusion.6 = f32[640,512]{1,0:T(8,128)S(1)} fusion(bf16[640,7168]{1,0:T(8,128)(2,1)S(1)} %bitcast.56, bf16[1,7168,512]{2,1,0:T(8,128)(2,1)} %param.9), kind=kOutput, calls=%fused_computation.14 | convolution fusion | flops 4697620480 | bytes 17825792 | tf_op jit(solution)/shard_map/dot_general | solution.py:15
  175.5 5.0 fusion.11
  180.5 7.3 %convolution_convert_fusion = bf16[640,7168]{1,0:T(8,128)(2,1)} fusion(bf16[640,512]{1,0:T(8,128)(2,1)S(1)} %fusion.11, bf16[1,512,7168]{2,1,0:T(8,128)(2,1)S(1)} %bitcast.66), kind=kOutput, calls=%fused_computation.6 | convolution fusion | flops 4702208000 | bytes 17170432 | tf_op jit(solution)/shard_map/dot_general | solution.py:18
  187.8 6.8 %all-to-all-start.3 = ((bf16[16,40,7168]{2,1,0:T(8,128)(2,1)}), bf16[16,40,7168]{2,1,0:T(8,128)(2,1)}, u32[]{:S(2)}, u32[]{:S(2)}) async-start(bf16[16,40,7168]{2,1,0:T(8,128)(2,1)} %bitcast.55), calls=%async_computation.3 | async-start | bytes 18350080 | tf_op jit(solution)/shard_map/all_to_all | solution.py:75
  194.6 0.1 copy.76
  194.9 141.9 %all-to-all-done.3 = bf16[16,40,7168]{2,1,0:T(8,128)(2,1)} async-done(((bf16[16,40,7168]{2,1,0:T(8,128)(2,1)}), bf16[16,40,7168]{2,1,0:T(8,128)(2,1)}, u32[]{:S(2)}, u32[]{:S(2)}) %all-to-all-start.3) | async-done | bytes 9175072 | tf_op jit(solution)/shard_map/all_to_all | solution.py:75
  336.8 8.1 %convert_reduce_fusion = f32[4,40,7168]{2,1,0:T(8,128)} fusion(bf16[16,40,7168]{2,1,0:T(8,128)(2,1)} %all-to-all-done.3), kind=kLoop, calls=%fused_computation.2 | loop fusion | flops 8028160 | bytes 13762560 | tf_op jit(solution)/shard_map/reduce_sum | solution.py:76
  344.9 48.6 %gather_fusion = f32[640,7168]{1,0:T(8,128)} fusion(f32[4,40,7168]{2,1,0:T(8,128)} %convert_reduce_fusion, s32[640]{0:T(1024)S(1)} %reshape.95), kind=kCustom, calls=%fused_computation | custom fusion | bytes 36705280 | tf_op jit(solution)/shard_map/gather | solution.py:80
  393.5 20.0 %reshape.98 = f32[160,4,7168]{2,1,0:T(4,128)} reshape(f32[640,7168]{1,0:T(8,128)} %gather_fusion) | data formatting | bytes 36700160 | tf_op jit(solution)/shard_map/gather | solution.py:80
  413.5 15.5 %multiply_reduce_fusion = bf16[160,7168]{1,0:T(8,128)(2,1)S(1)} fusion(f32[160,4,7168]{2,1,0:T(4,128)} %reshape.98, f32[160,4]{1,0:T(8,128)S(1)} %copy.76), kind=kLoop, calls=%fused_computation.3 | loop fusion | flops 8028160 | bytes 20646400 | tf_op jit(solution)/shard_map/reduce_sum | solution.py:81
  429.0 2.2 convert_element_type.81
  431.2 5.2 %all-to-all-start.4 = ((bf16[8,20,7168]{2,1,0:T(8,128)(2,1)}), bf16[8,20,7168]{2,1,0:T(8,128)(2,1)}, u32[]{:S(2)}, u32[]{:S(2)}) async-start(bf16[8,20,7168]{2,1,0:T(8,128)(2,1)} %convert_element_type.81), calls=%async_computation.4 | async-start | bytes 5505024 | tf_op jit(solution)/shard_map/all_to_all | solution.py:84
  436.6 34.1 %all-to-all-done.4 = bf16[8,20,7168]{2,1,0:T(8,128)(2,1)} async-done(((bf16[8,20,7168]{2,1,0:T(8,128)(2,1)}), bf16[8,20,7168]{2,1,0:T(8,128)(2,1)}, u32[]{:S(2)}, u32[]{:S(2)}) %all-to-all-start.4) | async-done | bytes 2293792 | tf_op jit(solution)/shard_map/all_to_all | solution.py:84
  470.7 5.2 %copy_convert_fusion = f32[8,20,7168]{2,0,1:T(8,128)} fusion(bf16[8,20,7168]{2,1,0:T(8,128)(2,1)} %all-to-all-done.4), kind=kLoop, calls=%fused_computation.16 | loop fusion | flops 1146880 | bytes 6881280 | tf_op jit(solution)/shard_map/convert_element_type | solution.py:86
  475.9 29.5 %gather_fusion.1 = f32[512,7168]{1,0:T(8,128)} fusion(f32[8,20,7168]{2,0,1:T(8,128)} %copy_convert_fusion, s32[512]{0:T(512)S(1)} %reshape.101), kind=kCustom, calls=%fused_computation.1 | custom fusion | bytes 29364224 | tf_op jit(solution)/shard_map/gather | solution.py:88
  505.3 11.6 %fusion = bf16[64,7168]{1,0:T(8,128)(2,1)} fusion(f32[512,7168]{1,0:T(8,128)} %gather_fusion.1, pred[64,8]{1,0:T(8,128)(4,1)S(1)} %copy.66), kind=kLoop, calls=%fused_computation.5 | loop fusion | flops 6881280 | bytes 15598080 | tf_op jit(solution)/shard_map/reduce_sum | solution.py:89
  (40 shorter events, 1.3 us)
Async XLA Ops:
  0.0 7.6 %copy-start = (bf16[64,7168]{1,0:T(8,128)(2,1)S(1)}, bf16[64,7168]{1,0:T(8,128)(2,1)}, u32[]{:S(2)}) copy-start(bf16[64,7168]{1,0:T(8,128)(2,1)} %param.6) | copy-start | bytes 2752516
  3.3 9.6 %all-to-all-start.1 = ((bf16[8,20,4]{1,2,0:T(4,128)(2,1)}), bf16[8,20,4]{1,2,0:T(4,128)(2,1)S(1)}, u32[]{:S(2)}, u32[]{:S(2)}) async-start(bf16[8,20,4]{1,2,0:T(4,128)(2,1)} %convolution_convert_fusion.3), calls=%async_computation.1 | async-start | bytes 16384 | tf_op jit(solution)/shard_map/all_to_all | solution.py:53
  12.9 38.6 %all-to-all-start = ((bf16[8,20,7168]{2,1,0:T(8,128)(2,1)}), bf16[8,20,7168]{2,1,0:T(8,128)(2,1)}, u32[]{:S(2)}, u32[]{:S(2)}) async-start(bf16[8,20,7168]{2,1,0:T(8,128)(2,1)} %copy.70), calls=%async_computation | async-start | bytes 5505024 | tf_op jit(solution)/shard_map/all_to_all | solution.py:52
  59.2 116.2 %slice-start = ((s8[7340032]{0:T(1024)(128)(4,1)}), s8[4194304]{0:T(1024)(128)(4,1)S(1)}, s32[]{:S(2)}) async-start(s8[7340032]{0:T(1024)(128)(4,1)} %bitcast.63), calls=%async_computation.5 | async-start | bytes 8388608
  168.0 7.5 %slice-start.1 = ((s8[7340032]{0:T(1024)(128)(4,1)}), s8[3145728]{0:T(1024)(128)(4,1)S(1)}, s32[]{:S(2)}) async-start(s8[7340032]{0:T(1024)(128)(4,1)} %bitcast.63), calls=%async_computation.6 | async-start | bytes 6291456
  168.0 12.5 %slice-start.2 = ((s8[7340032]{0:T(1024)(128)(4,1)}), s8[4194304]{0:T(1024)(128)(4,1)S(1)}, s32[]{:S(2)}) async-start(s8[7340032]{0:T(1024)(128)(4,1)} %bitcast.65), calls=%async_computation.7 | async-start | bytes 8388608
  175.5 5.1 slice-start.3
  187.8 149.0 %all-to-all-start.3 = ((bf16[16,40,7168]{2,1,0:T(8,128)(2,1)}), bf16[16,40,7168]{2,1,0:T(8,128)(2,1)}, u32[]{:S(2)}, u32[]{:S(2)}) async-start(bf16[16,40,7168]{2,1,0:T(8,128)(2,1)} %bitcast.55), calls=%async_computation.3 | async-start | bytes 18350080 | tf_op jit(solution)/shard_map/all_to_all | solution.py:75
  431.2 39.5 %all-to-all-start.4 = ((bf16[8,20,7168]{2,1,0:T(8,128)(2,1)}), bf16[8,20,7168]{2,1,0:T(8,128)(2,1)}, u32[]{:S(2)}, u32[]{:S(2)}) async-start(bf16[8,20,7168]{2,1,0:T(8,128)(2,1)} %convert_element_type.81), calls=%async_computation.4 | async-start | bytes 5505024 | tf_op jit(solution)/shard_map/all_to_all | solution.py:84
  475.9 41.1 %copy-start.1 = (bf16[64,7168]{1,0:T(8,128)(2,1)S(1)}, bf16[64,7168]{1,0:T(8,128)(2,1)}, u32[]{:S(2)}) copy-start(bf16[64,7168]{1,0:T(8,128)(2,1)} %param.6) | copy-start | bytes 2752516
where the time goes:
time: 523 us; the launch traced here: 517 us
  waiting for transfers between devices  210 us (40%)
  local copies, waits for them, and re-layouts  110 us (21%)
  blocking collectives  109 us (21%)
  other arithmetic  44.2 us (8%)
  matrix products  23.4 us (4%)
  starting transfers between devices  20.7 us (4%)
    all_to_all x1, waiting for transfers between devices, per_device(): lax.all_to_all(results, 'local', split_axis=0, concat_axis=0, tiled=True)  142 us
    all_to_all x1, blocking collectives, per_device(): lax.all_to_all(outgoing, 'local', split_axis=0, concat_axis=0, tiled=True)  109 us
    gather x2, local copies, waits for them, and re-layouts, per_device(): gathered = summed[local_ids[None, :], jnp.clip(position, 0, capacity - 1)]  68.6 us
    all_to_all x1, waiting for transfers between devices, per_device(): lax.all_to_all(node_total.astype(jnp.bfloat16), 'node', split_axis=0, con...  34.1 us
    all_to_all x1, waiting for transfers between devices, per_device(): lax.all_to_all(send_rows, 'node', split_axis=0, concat_axis=0, tiled=True)  32.2 us
    gather x1, local copies, waits for them, and re-layouts, per_device(): returned_home[node_ids[None, :], jnp.clip(node_slot, 0, node_cap - 1)]  29.5 us
    reduce_sum x1, other arithmetic, per_device(): jnp.sum(gathered * row_weight[:, :, None], axis=1)  15.5 us
    reduce_sum x1, other arithmetic, per_device(): jnp.sum(jnp.where(reached[:, :, None], gathered_home, 0.0), axis=1)  11.6 us
  transfers between devices with their start and end apart: 4, of which 4 were waited for; matrix products, arithmetic and copies ran while one was open for 1% of the time, Pallas kernels for 0%

commit v1 on v0

v1 whole, which is shorter than its diff:
```python
import jax
import jax.numpy as jnp
from jax import lax
from jax.sharding import Mesh, PartitionSpec as P

SCALE = 2.827
SLOTS = 5
AXES = ("x", "core", "y", "z")
BF = jnp.bfloat16
F32 = jnp.float32


def dot(a, b):
    return jnp.dot(a, b, preferred_element_type=F32)


def per_device(tokens, routes, scores, gate_proj, up_proj, down_proj):
    count, width = tokens.shape
    parts = 8
    piece = width // parts
    experts = 32
    group = parts * SLOTS
    weights = (SCALE * scores / jnp.sum(scores, axis=1, keepdims=True)).astype(BF)
    labels = jnp.arange(experts, dtype=jnp.int32)
    hits = routes[:, :, None] == labels[None, None, :]
    member = jnp.any(hits, axis=1)
    dense = jnp.sum(jnp.where(hits, weights[:, :, None].astype(F32), 0.0), axis=1)
    earlier = (jnp.arange(count)[:, None] > jnp.arange(count)[None, :]).astype(BF)
    rank = dot(earlier, member.astype(BF))
    slot = jnp.arange(SLOTS, dtype=F32)
    pick = (member.T[:, None, :] & (rank.T[:, None, :] == slot[None, :, None])).astype(BF)
    eye = jnp.eye(parts, dtype=BF)
    pick_parts = (pick[:, None, :, None, :] * eye[None, :, None, :, None]).reshape(
        experts * group, parts * count
    )
    stacked = tokens.reshape(count, parts, piece).transpose(1, 0, 2).reshape(parts * count, piece)
    send = dot(pick_parts, stacked).astype(BF).reshape(experts, 1, group, piece)
    send = jnp.broadcast_to(send, (experts, 4, group, piece)).reshape(experts * 4, group, piece)
    came = lax.all_to_all(send, AXES, 0, 0, tiled=True)
    near = 8
    far = experts * 4 // near
    src = jnp.arange(near * group)
    place = (src // SLOTS) % parts * (near * SLOTS) + src // group * SLOTS + src % SLOTS
    unmix = (place[None, :] == jnp.arange(near * group)[:, None]).astype(BF)
    rows = jnp.einsum("ab,gbn->gan", unmix, came.reshape(far, near * group, piece),
                      preferred_element_type=F32).astype(BF)
    rows = rows.reshape(far, parts, near * SLOTS, piece).transpose(0, 2, 1, 3)
    rows = rows.reshape(far * near * SLOTS, width)
    gate = dot(rows, gate_proj[0])
    up = dot(rows, up_proj[0])
    hidden = (jax.nn.silu(gate) * up).astype(BF)
    partial = dot(hidden, down_proj[0]).astype(BF)
    back = partial.reshape(far, near * SLOTS, parts, piece).transpose(0, 2, 1, 3)
    back = jnp.einsum("ba,gbn->gan", unmix, back.reshape(far, near * group, piece),
                      preferred_element_type=F32).astype(BF)
    home = lax.all_to_all(back.reshape(experts * 4, group, piece), AXES, 0, 0, tiled=True)
    share = pick.astype(F32) * dense.T[:, None, :]
    share = jnp.broadcast_to(
        share.transpose(2, 0, 1)[None, :, :, None, None, :]
        * jnp.eye(parts, dtype=F32)[:, None, None, None, :, None],
        (parts, count, experts, 4, parts, SLOTS),
    ).reshape(parts * count, experts * 4 * group).astype(BF)
    out = dot(share, home.reshape(experts * 4 * group, piece)).astype(BF)
    return out.reshape(parts, count, piece).transpose(1, 0, 2).reshape(count, width)


def solution(mesh):
    grid = Mesh(mesh.devices.reshape(4, 2, 4, 4), AXES)
    return jax.shard_map(
        per_device,
        mesh=grid,
        in_specs=(P(AXES, None), P(AXES, None), P(AXES, None), P(AXES, None, None), P(AXES, None, None), P(AXES, None, None)),
        out_specs=P(AXES, None),
        check_vma=False,
    )
```

time: 523 us -> 376 us (0.72); the launches traced: 517 us -> 375 us
  blocking collectives: 109 us -> 0 us
  other arithmetic: 44.2 us -> 2.41 us
  matrix products: 23.4 us -> 62.1 us
  local copies, waits for them, and re-layouts: 110 us -> 75.2 us
  waiting for transfers between devices: 210 us -> 219 us
    all_to_all x1 -> x0, blocking collectives: 109 us -> none  [per_device(): lax.all_to_all(outgoing, 'local', split_axis=0, concat_axis=0, tiled=True)]
    gather x3 -> x0, local copies, waits for them, and re-layouts: 98 us -> none  [the longest x2 68.6 us: per_device(): gathered = summed[local_ids[None, :], jnp.clip(position, 0, capacity - 1)]]
    dot_general x6 -> x8, matrix products: 23.4 us -> 62.1 us  [the longest x6 38.9 us: dot(): return jnp.dot(a, b, preferred_element_type=F32)]
    reduce_sum x4 -> x1, other arithmetic: 35.9 us -> 0.01 us  [per_device(): jnp.sum(jnp.where(hits, weights[:, :, None].astype(F32), 0.0), axis=1)]
    unnamed x12 -> x17, local copies, waits for them, and re-layouts: 0.03 us -> 20 us
    transpose x0 -> x3, local copies, waits for them, and re-layouts: none -> 16.7 us  [the longest x2 16.6 us: per_device(): partial.reshape(far, near * SLOTS, parts, piece).transpose(0, 2, 1, 3)]
    convert_element_type x5 -> x2, local copies, waits for them, and re-layouts: 5.36 us -> 15.3 us  [the longest x1 14.6 us: per_device(): share = jnp.broadcast_to(share.transpose(2, 0, 1)[None, :, :, None, None,...]
    all_to_all x4 -> x2, waiting for transfers between devices: 210 us -> 219 us  [the longest x1 118 us: per_device(): came = lax.all_to_all(send, AXES, 0, 0, tiled=True)]
  transfers between devices with their start and end apart: 4 -> 2, of which waited for: 4 -> 2; matrix products, arithmetic and copies ran while one was open for 1% -> 6% of each run, Pallas kernels for 0% -> 0%
where the time goes in v1:
time: 376 us; the launch traced here: 375 us
  waiting for transfers between devices  219 us (58%)
  local copies, waits for them, and re-layouts  75.2 us (20%)
  matrix products  62.1 us (17%)
  starting transfers between devices  16.5 us (4%)
    all_to_all x1, waiting for transfers between devices, per_device(): came = lax.all_to_all(send, AXES, 0, 0, tiled=True)  118 us
    all_to_all x1, waiting for transfers between devices, per_device(): lax.all_to_all(back.reshape(experts * 4, group, piece), AXES, 0, 0, tiled...  101 us
    dot_general x6, matrix products, dot(): return jnp.dot(a, b, preferred_element_type=F32)  38.9 us
    unnamed x17, local copies, waits for them, and re-layouts  20 us
    transpose x2, local copies, waits for them, and re-layouts, per_device(): partial.reshape(far, near * SLOTS, parts, piece).transpose(0, 2, 1, 3)  16.6 us
    convert_element_type x1, local copies, waits for them, and re-layouts, per_device(): share = jnp.broadcast_to(share.transpose(2, 0, 1)[None, :, :, None, None,...  14.6 us
    dot_general x1, matrix products, per_device(): jnp.einsum('ab,gbn->gan', unmix, came.reshape(far, near * group, piece),...  12.3 us
    dot_general x1, matrix products, per_device(): jnp.einsum('ba,gbn->gan', unmix, back.reshape(far, near * group, piece),...  11 us
  transfers between devices with their start and end apart: 2, of which 2 were waited for; matrix products, arithmetic and copies ran while one was open for 6% of the time, Pallas kernels for 0%

profile of v1, /device:TPU:96, one launch (start us, length us, event | category | flops | bytes accessed | tf_op | source)
XLA Modules:
  0.0 375.3 jit_solution(13802787513217862167)
XLA Ops:
  0.0 0.7 copy.29
  0.7 0.7 fusion.20
  1.4 0.0 copy-start.1
  1.4 0.1 fusion.21
  1.5 1.3 copy.38
  2.8 0.1 copy.30
  3.0 0.9 broadcast_multiply_fusion
  3.9 2.4 mul.99
  6.3 2.8 convolution_convert_fusion.3
  9.2 4.2 %broadcast_in_dim.22 = bf16[32,4,40,896]{3,2,1,0:T(8,128)(2,1)} broadcast(bf16[32,40,896]{2,1,0:T(8,128)(2,1)S(1)} %bitcast.78), dimensions={0,2,3} | broadcast | bytes 11468800 | tf_op jit(solution)/shard_map/broadcast_in_dim | solution.py:38
  13.4 10.3 %all-to-all-start = ((bf16[128,40,896]{2,1,0:T(8,128)(2,1)}), bf16[128,40,896]{2,1,0:T(8,128)(2,1)}, u32[]{:S(2)}, u32[]{:S(2)}) async-start(bf16[128,40,896]{2,1,0:T(8,128)(2,1)} %bitcast.71), calls=%async_computation | async-start | bytes 18350080 | tf_op jit(solution)/shard_map/all_to_all | solution.py:39
  23.7 118.2 %all-to-all-done = bf16[128,40,896]{2,1,0:T(8,128)(2,1)} async-done(((bf16[128,40,896]{2,1,0:T(8,128)(2,1)}), bf16[128,40,896]{2,1,0:T(8,128)(2,1)}, u32[]{:S(2)}, u32[]{:S(2)}) %all-to-all-start) | async-done | bytes 9175072 | tf_op jit(solution)/shard_map/all_to_all | solution.py:39
  141.9 12.3 %convolution_convert_fusion.2 = bf16[16,896,320]{1,2,0:T(8,128)(2,1)} fusion(bf16[16,320,896]{2,1,0:T(8,128)(2,1)} %bitcast.6, s32[320]{0:T(512)S(1)} %fusion.30), kind=kOutput, calls=%fused_computation.8 | convolution fusion | flops 2940702720 | bytes 18351360 | tf_op jit(solution)/shard_map/ab,gbn->gan/dot_general | solution.py:45
  154.2 8.9 %copy.32 = bf16[16,8,40,896]{3,1,2,0:T(8,128)(2,1)} copy(bf16[16,8,40,896]{3,2,1,0:T(8,128)(2,1)} %bitcast.68) | data formatting | bytes 18350080 | tf_op jit(solution)/shard_map/reshape | solution.py:47
  163.1 9.3 %copy.39 = bf16[80,8,8,896]{3,1,2,0:T(8,128)(2,1)} copy(bf16[80,8,8,896]{3,2,1,0:T(8,128)(2,1)} %bitcast.72) | data formatting | bytes 18350080
  172.4 9.9 %fusion.3 = f32[640,512]{1,0:T(8,128)S(1)} fusion(bf16[640,7168]{1,0:T(8,128)(2,1)} %bitcast.74, bf16[1,7168,512]{2,1,0:T(8,128)(2,1)} %param.9), kind=kOutput, calls=%fused_computation.5 | convolution fusion | flops 4697620480 | bytes 17825792 | tf_op jit(solution)/shard_map/dot_general | solution.py:14
  182.3 0.0 copy-done
  182.3 0.0 slice-start.1
  182.3 8.3 %fusion.8 = bf16[640,512]{1,0:T(8,128)(2,1)S(1)} fusion(bf16[640,7168]{1,0:T(8,128)(2,1)S(1)} %bitcast.75, bf16[1,7168,512]{2,1,0:T(8,128)(2,1)} %param.10, f32[640,512]{1,0:T(8,128)S(1)} %fusion.3), kind=kOutput, calls=%fused_computation.13 | convolution fusion | flops 4699586560 | bytes 18481152 | tf_op jit(solution)/shard_map/dot_general | solution.py:14
  190.6 0.0 slice-done
  190.6 7.5 %convolution_convert_fusion = bf16[640,7168]{1,0:T(8,128)(2,1)} fusion(bf16[640,512]{1,0:T(8,128)(2,1)S(1)} %fusion.8, bf16[1,512,7168]{2,1,0:T(8,128)(2,1)S(1)} %bitcast.85), kind=kOutput, calls=%fused_computation | convolution fusion | flops 4702208000 | bytes 17170432 | tf_op jit(solution)/shard_map/dot_general | solution.py:14
  198.1 9.3 %copy.40 = bf16[80,8,8,896]{3,2,1,0:T(8,128)(2,1)} copy(bf16[80,8,8,896]{3,1,2,0:T(8,128)(2,1)} %bitcast.76) | data formatting | bytes 18350080
  207.4 7.9 %bitcast_bitcast_fusion = bf16[16,8,40,896]{3,1,2,0:T(8,128)(2,1)} fusion(bf16[16,40,8,896]{3,2,1,0:T(8,128)(2,1)} %bitcast.73), kind=kLoop, calls=%fused_computation.1 | loop fusion | bytes 18350080 | tf_op jit(solution)/shard_map/transpose | solution.py:53
  215.3 8.7 %copy.33 = bf16[16,8,40,896]{3,2,1,0:T(8,128)(2,1)} copy(bf16[16,8,40,896]{3,1,2,0:T(8,128)(2,1)} %bitcast_bitcast_fusion) | data formatting | bytes 18350080 | tf_op jit(solution)/shard_map/transpose | solution.py:53
  224.0 11.0 %convolution_convert_fusion.1 = bf16[16,896,320]{1,2,0:T(8,128)(2,1)} fusion(bf16[16,320,896]{2,1,0:T(8,128)(2,1)} %bitcast.70, s32[320]{0:T(512)S(1)} %fusion.30), kind=kOutput, calls=%fused_computation.7 | convolution fusion | flops 2940702720 | bytes 18351360 | tf_op jit(solution)/shard_map/ba,gbn->gan/dot_general | solution.py:54
  235.0 6.2 %all-to-all-start.1 = ((bf16[128,40,896]{2,1,0:T(8,128)(2,1)}), bf16[128,40,896]{2,1,0:T(8,128)(2,1)}, u32[]{:S(2)}, u32[]{:S(2)}) async-start(bf16[128,40,896]{2,1,0:T(8,128)(2,1)} %bitcast.69), calls=%async_computation.1 | async-start | bytes 18350080 | tf_op jit(solution)/shard_map/all_to_all | solution.py:56
  241.4 0.7 multiply_convert_fusion
  242.1 6.6 %broadcast_in_dim.20 = bf16[8,64,32,4,8,5]{1,0,5,4,3,2:T(8,128)(2,1)} broadcast(bf16[8,64,32,8,5]{1,0,4,3,2:T(8,128)(2,1)S(1)} %multiply_convert_fusion), dimensions={0,1,2,4,5} | broadcast | bytes 6553600 | tf_op jit(solution)/shard_map/broadcast_in_dim | solution.py:58
  248.7 14.6 %convert_element_type.83 = bf16[512,5120]{0,1:T(8,128)(2,1)} reshape(bf16[8,64,32,4,8,5]{1,0,5,4,3,2:T(8,128)(2,1)} %broadcast_in_dim.20) | data formatting | bytes 10485760 | tf_op jit(solution)/shard_map/convert_element_type | solution.py:62
  263.3 100.7 %all-to-all-done.1 = bf16[128,40,896]{2,1,0:T(8,128)(2,1)} async-done(((bf16[128,40,896]{2,1,0:T(8,128)(2,1)}), bf16[128,40,896]{2,1,0:T(8,128)(2,1)}, u32[]{:S(2)}, u32[]{:S(2)}) %all-to-all-start.1) | async-done | bytes 9175072 | tf_op jit(solution)/shard_map/all_to_all | solution.py:56
  364.0 10.3 %convolution_convert_fusion.4 = bf16[512,896]{1,0:T(8,128)(2,1)S(1)} fusion(bf16[512,5120]{0,1:T(8,128)(2,1)} %convert_element_type.83, bf16[5120,896]{1,0:T(8,128)(2,1)} %bitcast.19), kind=kOutput, calls=%fused_computation.12 | convolution fusion | flops 4698079232 | bytes 15335424 | tf_op jit(solution)/shard_map/dot_general | solution.py:14
  374.2 1.1 copy.37
  (19 shorter events, 0.2 us)
Async XLA Ops:
  1.4 1.6 copy-start.1
  13.4 128.5 %all-to-all-start = ((bf16[128,40,896]{2,1,0:T(8,128)(2,1)}), bf16[128,40,896]{2,1,0:T(8,128)(2,1)}, u32[]{:S(2)}, u32[]{:S(2)}) async-start(bf16[128,40,896]{2,1,0:T(8,128)(2,1)} %bitcast.71), calls=%async_computation | async-start | bytes 18350080 | tf_op jit(solution)/shard_map/all_to_all | solution.py:39
  172.4 9.9 %copy-start = (bf16[80,8,8,896]{3,1,2,0:T(8,128)(2,1)S(1)}, bf16[80,8,8,896]{3,1,2,0:T(8,128)(2,1)}, u32[]{:S(2)}) copy-start(bf16[80,8,8,896]{3,1,2,0:T(8,128)(2,1)} %copy.39) | copy-start | bytes 27525124
  172.4 18.2 %slice-start = ((s8[7340032]{0:T(1024)(128)(4,1)}), s8[4194304]{0:T(1024)(128)(4,1)S(1)}, s32[]{:S(2)}) async-start(s8[7340032]{0:T(1024)(128)(4,1)} %bitcast.84), calls=%async_computation.2 | async-start | bytes 8388608
  182.3 8.3 %slice-start.1 = ((s8[7340032]{0:T(1024)(128)(4,1)}), s8[3145728]{0:T(1024)(128)(4,1)S(1)}, s32[]{:S(2)}) async-start(s8[7340032]{0:T(1024)(128)(4,1)} %bitcast.84), calls=%async_computation.3 | async-start | bytes 6291456
  235.0 6.2 %copy-start.4 = (f32[64,2]{0,1:T(2,128)S(1)}, f32[64,2]{0,1:T(2,128)}, u32[]{:S(2)}) copy-start(f32[64,2]{0,1:T(2,128)} %param.8) | copy-start | bytes 1540
  235.0 6.3 %copy-start.3 = (s32[64,2]{0,1:T(2,128)S(1)}, s32[64,2]{0,1:T(2,128)}, u32[]{:S(2)}) copy-start(s32[64,2]{0,1:T(2,128)} %param.7) | copy-start | bytes 1540
  235.0 6.3 %copy-start.2 = (pred[64,32]{0,1:T(8,128)(4,1)S(1)}, pred[64,32]{0,1:T(8,128)(4,1)}, u32[]{:S(2)}) copy-start(pred[64,32]{0,1:T(8,128)(4,1)} %copy-done.1) | copy-start | bytes 6148
  235.0 128.9 %all-to-all-start.1 = ((bf16[128,40,896]{2,1,0:T(8,128)(2,1)}), bf16[128,40,896]{2,1,0:T(8,128)(2,1)}, u32[]{:S(2)}, u32[]{:S(2)}) async-start(bf16[128,40,896]{2,1,0:T(8,128)(2,1)} %bitcast.69), calls=%async_computation.1 | async-start | bytes 18350080 | tf_op jit(solution)/shard_map/all_to_all | solution.py:56

commit v2 on v1

v2 whole, which is shorter than its diff:
```python
import functools

import jax
import jax.numpy as jnp
from jax import lax
from jax.experimental import pallas as pl
from jax.experimental.pallas import tpu as pltpu
from jax.sharding import Mesh, PartitionSpec as P


SCALE = 2.827
SLOTS = 5
AXES = ("x", "core", "y", "z")
PLANE = ("x", "core", "y")
BF = jnp.bfloat16
F32 = jnp.float32
TOK = 64
EXPERTS = 32
HID = 512
FIRST = 3072
SECOND = 4096
PARTS = 8
PIECE = SECOND // PARTS
SENT = EXPERTS * PARTS * SLOTS
CHIPS = 16
BLOCKS = 8
CHUNK = BLOCKS * SLOTS
ROWS = CHIPS * CHUNK
QUARTER = ROWS // 4
STRIP = QUARTER // 2
HALF = ROWS // 2
FACTS = 128
TILE = 1024
STEP = 256


def dot(a, b):
    return jnp.dot(a, b, preferred_element_type=F32)


def cost(flops, nbytes):
    return pl.CostEstimate(flops=flops, bytes_accessed=nbytes, transcendentals=0)


def whole(*shape):
    return pl.BlockSpec(shape, lambda *_: (0,) * len(shape))


def column(rows, tile=TILE, skip=0):
    return pl.BlockSpec((rows, tile), lambda j: (0, j + skip))


def each(width, step, body):
    def run(i, carry):
        body(pl.ds(pl.multiple_of(i * step, step), step))
        return carry

    lax.fori_loop(0, width // step, run, 0)


def iota(shape, axis):
    return lax.broadcasted_iota(jnp.int32, shape, axis)


def flip(rows):
    unit = (iota((TOK, TOK), 0) == iota((TOK, TOK), 1)).astype(BF)
    return lax.dot_general(unit, rows.astype(BF), (((1,), (1,)), ((), ())), preferred_element_type=F32)


def routing(routes, scores):
    expert = routes.astype(F32)
    label = iota((EXPERTS, TOK), 0).astype(F32)
    hits = [(expert[k:k + 1] == label).astype(F32) for k in range(2)]
    earlier = (iota((TOK, TOK), 0) < iota((TOK, TOK), 1)).astype(BF)
    rank = dot((hits[0] + hits[1]).astype(BF), earlier)
    slots = [jnp.sum(hits[k] * rank, axis=0, keepdims=True) for k in range(2)]
    codes = expert * SLOTS + jnp.concatenate(slots, axis=0)
    weights = (SCALE * scores / (scores[0:1] + scores[1:2])).astype(BF)
    return codes, weights


def send_body(tokens_ref, routes_ref, scores_ref, own_ref, send_ref, pick_ref):
    codes, weights = routing(routes_ref[...], scores_ref[...])
    own_ref[:, :FIRST] = tokens_ref[:, :FIRST]
    lane = iota((TOK, FACTS), 1)
    facts = jnp.zeros((TOK, FACTS), F32)
    for at, columns in ((0, flip(codes)), (2, flip(weights))):
        for k in range(2):
            facts = jnp.where(lane == at + k, columns[:, k:k + 1], facts)
    own_ref[:, FIRST:] = facts.astype(BF)
    lanes = PARTS * TOK
    spread = (iota((TOK, lanes), 1) % TOK == iota((TOK, lanes), 0)).astype(BF)
    across = dot(codes.astype(BF), spread)
    row = iota((SENT, 1), 0)
    code = (row // (PARTS * SLOTS) * SLOTS + row % SLOTS).astype(F32)
    part = row // SLOTS % PARTS
    fits = ((code == across[0:1]) | (code == across[1:2])) & (part == iota((1, lanes), 1) // TOK)
    pick_ref[...] = jnp.where(fits, 1.0, 0.0).astype(BF)
    stacked = jnp.concatenate(
        [tokens_ref[:, FIRST + i * PIECE:FIRST + (i + 1) * PIECE] for i in range(PARTS)], axis=0
    )

    def body(rows):
        send_ref[rows, :] = dot(pick_ref[rows, :], stacked).astype(BF)

    each(SENT, 320, body)


def send(tokens, routes, scores):
    return pl.pallas_call(
        send_body,
        out_shape=[
            jax.ShapeDtypeStruct((TOK, FIRST + FACTS), BF),
            jax.ShapeDtypeStruct((SENT, PIECE), BF),
        ],
        scratch_shapes=[pltpu.VMEM((SENT, PARTS * TOK), BF)],
        cost_estimate=cost(2 * SENT * PARTS * TOK * PIECE, 3_000_000),
    )(tokens, routes, scores)


def chunk_code(shape, axis):
    at = iota(shape, axis)
    chip = at // CHUNK
    expert = (chip // 4 * 2 + lax.axis_index("core")) * 4 + chip % 4
    return (expert * SLOTS + at % SLOTS).astype(F32), at % CHUNK // SLOTS


def select_body(*refs):
    tokens, facts, (out, pick) = refs[:BLOCKS], refs[BLOCKS:2 * BLOCKS], refs[2 * BLOCKS:]

    @pl.when(pl.program_id(0) == 0)
    def _():
        stacked = jnp.concatenate([r[...] for r in facts], axis=0)
        unit = (iota((8, FACTS), 0) == iota((8, FACTS), 1)).astype(BF)
        codes = lax.dot_general(unit, stacked, (((1,), (1,)), ((), ())), preferred_element_type=F32)
        code, block = chunk_code((ROWS, 1), 0)
        fits = ((code == codes[0:1]) | (code == codes[1:2])) & (block == iota((1, BLOCKS * TOK), 1) // TOK)
        pick[...] = jnp.where(fits, 1.0, 0.0).astype(BF)

    def body(cols):
        out[:, cols] = dot(pick[...], jnp.concatenate([r[:, cols] for r in tokens], axis=0)).astype(BF)

    each(TILE, STEP, body)


FACT_SPEC = pl.BlockSpec((TOK, FACTS), lambda j: (0, FIRST // FACTS))


def select(blocks):
    return pl.pallas_call(
        select_body,
        grid=(FIRST // TILE,),
        in_specs=[column(TOK)] * BLOCKS + [FACT_SPEC] * BLOCKS,
        out_specs=column(ROWS),
        out_shape=jax.ShapeDtypeStruct((ROWS, FIRST), BF),
        scratch_shapes=[pltpu.VMEM((ROWS, BLOCKS * TOK), BF)],
        cost_estimate=cost(2 * ROWS * BLOCKS * TOK * FIRST, 8_000_000),
    )(*blocks, *blocks)


def accumulate(rows, gate_w, up_w, gate, up):
    @pl.when(pl.program_id(0) == 0)
    def _():
        gate[...] = jnp.zeros_like(gate)
        up[...] = jnp.zeros_like(up)

    def body(cols):
        gate[:, cols] += dot(rows, gate_w[:, cols])
        up[:, cols] += dot(rows, up_w[:, cols])

    each(HID, STEP, body)


def gate_up_body(count, *refs):
    accumulate(jnp.concatenate([r[...] for r in refs[:count]], axis=0), *refs[count:])


def weight_tile(skip):
    return pl.BlockSpec((TILE, HID), lambda k: (k + skip, 0))


def gate_up(blocks, gate_w, up_w):
    count = len(blocks)
    high = blocks[0].shape[0]
    rows = high * count
    return pl.pallas_call(
        functools.partial(gate_up_body, count),
        grid=(SECOND // TILE,),
        in_specs=[column(high)] * count + [weight_tile(FIRST // TILE)] * 2,
        out_specs=[whole(rows, HID)] * 2,
        out_shape=[jax.ShapeDtypeStruct((rows, HID), F32)] * 2,
        cost_estimate=cost(4 * rows * SECOND * HID, 12_000_000),
    )(*blocks, gate_w, up_w)


def hidden_body(mix_ref, rows_ref, gate_w, up_w, gate_n, up_n, gate_f, up_f, out, gate, up):
    rows = [dot(mix_ref[...], rows_ref[h * HALF:(h + 1) * HALF]).astype(BF) for h in range(2)]
    accumulate(jnp.concatenate(rows, axis=0), gate_w, up_w, gate, up)

    @pl.when(pl.program_id(0) == pl.num_programs(0) - 1)
    def _():
        for k in range(4):
            for h in range(2):
                at, mixed = k * QUARTER + h * STRIP, h * HALF + k * STRIP
                place = (0, 1, None, 2)[k]
                g_ref, u_ref = (gate_f, up_f) if place is None else (gate_n, up_n)
                off = h * STRIP + (place or 0) * QUARTER
                g = gate[mixed:mixed + STRIP] + g_ref[off:off + STRIP]
                u = up[mixed:mixed + STRIP] + u_ref[off:off + STRIP]
                out[at:at + STRIP] = (g / (1.0 + jnp.exp(-g)) * u).astype(BF)


def hidden_of(mix, rows, gate_w, up_w, near, far):
    return pl.pallas_call(
        hidden_body,
        grid=(FIRST // TILE,),
        in_specs=[whole(HALF, HALF), column(ROWS)] + [weight_tile(0)] * 2
        + [whole(3 * QUARTER, HID)] * 2 + [whole(QUARTER, HID)] * 2,
        out_specs=whole(ROWS, HID),
        out_shape=jax.ShapeDtypeStruct((ROWS, HID), BF),
        scratch_shapes=[pltpu.VMEM((ROWS, HID), F32)] * 2,
        cost_estimate=cost(2 * ROWS * FIRST * (2 * HID + HALF), 12_000_000),
    )(mix, rows, gate_w, up_w, *near, *far)


SPANS = ((0, QUARTER), (QUARTER, QUARTER), (2 * QUARTER, STRIP), (2 * QUARTER + STRIP, STRIP), (3 * QUARTER, QUARTER))


def down_quarters_body(hidden_ref, w_ref, *outs):
    def body(cols):
        rows = dot(hidden_ref[...], w_ref[:, cols]).astype(BF)
        for (at, size), out in zip(SPANS, outs):
            out[:, cols] = rows[at:at + size]

    each(TILE, STEP, body)


def down_quarters(hidden, w_down):
    return pl.pallas_call(
        down_quarters_body,
        grid=(SECOND // TILE,),
        in_specs=[whole(ROWS, HID), column(HID, skip=FIRST // TILE)],
        out_specs=[column(size) for _, size in SPANS],
        out_shape=[jax.ShapeDtypeStruct((size, SECOND), BF) for _, size in SPANS],
        cost_estimate=cost(2 * ROWS * HID * SECOND, 10_000_000),
    )(hidden, w_down)


def down_chunks_body(unmix_ref, hidden_ref, w_ref, out, mixed):
    @pl.when(pl.program_id(0) == 0)
    def _():
        for h in range(2):
            strips = [hidden_ref[k * QUARTER + h * STRIP:k * QUARTER + (h + 1) * STRIP] for k in range(4)]
            mixed[h * HALF:(h + 1) * HALF] = dot(unmix_ref[...], jnp.concatenate(strips, axis=0)).astype(BF)

    def body(cols):
        out[:, cols] = dot(mixed[...], w_ref[:, cols]).astype(BF)

    each(TILE, STEP, body)


def down_chunks(unmix, hidden, w_down):
    return pl.pallas_call(
        down_chunks_body,
        grid=(FIRST // TILE,),
        in_specs=[whole(HALF, HALF), whole(ROWS, HID), column(HID)],
        out_specs=column(ROWS),
        out_shape=jax.ShapeDtypeStruct((ROWS, FIRST), BF),
        scratch_shapes=[pltpu.VMEM((ROWS, HID), BF)],
        cost_estimate=cost(2 * ROWS * HID * FIRST, 8_000_000),
    )(unmix, hidden, w_down)


def combine_body(rows_ref, *refs):
    facts, (own, other, share) = refs[:BLOCKS], refs[BLOCKS:]
    half = own.shape[0]

    @pl.when(pl.program_id(0) == 0)
    def _():
        code, block = chunk_code((1, ROWS), 1)
        for b, ref in enumerate(facts):
            fact = ref[...].astype(F32)
            value = jnp.where(fact[:, 0:1] == code, fact[:, 2:3], 0.0) + jnp.where(
                fact[:, 1:2] == code, fact[:, 3:4], 0.0
            )
            at = (b % 2 * 4 + b // 2) * TOK
            share[at:at + TOK] = jnp.where(block == b, value, 0.0).astype(BF)

    def body(cols):
        rows = dot(share[...], rows_ref[:, cols])
        own[:, cols] = rows[:half]
        other[:, cols] = rows[half:].astype(BF)

    each(TILE, STEP, body)


def combine(rows, blocks):
    half = BLOCKS * TOK // 2
    return pl.pallas_call(
        combine_body,
        grid=(FIRST // TILE,),
        in_specs=[column(ROWS)] + [FACT_SPEC] * BLOCKS,
        out_specs=[column(half)] * 2,
        out_shape=[jax.ShapeDtypeStruct((half, FIRST), F32), jax.ShapeDtypeStruct((half, FIRST), BF)],
        scratch_shapes=[pltpu.VMEM((2 * half, ROWS), BF)],
        cost_estimate=cost(4 * ROWS * half * FIRST, 10_000_000),
    )(rows, *blocks)


def finish_body(home_ref, routes_ref, scores_ref, kept, a_ref, b_ref, c_ref, out, portion):
    left = kept[...] + a_ref[...].astype(F32) + b_ref[...].astype(F32) + c_ref[...].astype(F32)
    out[:, :FIRST] = left.astype(BF)
    codes, weights = routing(routes_ref[...], scores_ref[...])
    codes, worth = flip(codes), flip(weights)
    lane = iota((1, SENT), 1)
    code = (lane // (PARTS * SLOTS) * SLOTS + lane % SLOTS).astype(F32)
    value = jnp.where(codes[:, 0:1] == code, worth[:, 0:1], 0.0) + jnp.where(
        codes[:, 1:2] == code, worth[:, 1:2], 0.0
    )
    for i in range(PARTS):
        portion[i * TOK:(i + 1) * TOK] = jnp.where(lane // SLOTS % PARTS == i, value, 0.0).astype(BF)
    rows = dot(portion[...], home_ref[...]).astype(BF)
    for i in range(PARTS):
        out[:, FIRST + i * PIECE:FIRST + (i + 1) * PIECE] = rows[i * TOK:(i + 1) * TOK]


def finish(home, routes, scores, kept, parts):
    return pl.pallas_call(
        finish_body,
        out_shape=jax.ShapeDtypeStruct((TOK, FIRST + SECOND), BF),
        scratch_shapes=[pltpu.VMEM((PARTS * TOK, SENT), BF)],
        cost_estimate=cost(2 * SENT * PARTS * TOK * PIECE, 5_000_000),
    )(home, routes, scores, kept, *parts)


def along(x, step):
    return lax.ppermute(x, "z", [(i, (i + step) % 4) for i in range(4)])


def swap(x):
    return lax.ppermute(x, "core", [(0, 1), (1, 0)])


def same(a, b):
    return functools.reduce(jnp.logical_and, [p[:, None] == q[None, :] for p, q in zip(a, b)])


def per_device(tokens, routes, scores, gate_proj, up_proj, down_proj):
    core = lax.axis_index("core")
    w_gate, w_up, w_down = gate_proj[0], up_proj[0], down_proj[0]

    own, sending = send(tokens, routes.T, scores.T)
    planes = [own] + [None] * 3
    for step in (1, 3, 2):
        planes[step] = along(own, step)
    came = lax.all_to_all(sending.reshape(EXPERTS, PARTS * SLOTS, PIECE), PLANE, 0, 0, tiled=True)
    twins = []
    for k in range(4):
        twins.append(swap(planes[k]))
    blocks = [b for pair in zip(planes, twins) for b in pair]

    flat = jnp.arange(PARTS * QUARTER)
    here = flat % QUARTER
    chip = here // (2 * SLOTS)
    target = (flat // QUARTER, chip // 4, chip % 4, (core + here // SLOTS) % 2, here % SLOTS)
    src = flat // (PARTS * SLOTS)
    origin = (flat // SLOTS % PARTS, src // 8, src % 4, src // 4 % 2, flat % SLOTS)
    sort = same(target, origin).astype(BF)
    unsort = same(origin, target).astype(BF)

    flat = jnp.arange(HALF)
    placed = (flat // STRIP, flat % STRIP // 10, flat % 10)
    landed = (flat % CHUNK // 10, flat // CHUNK, flat % 10)
    mix = same(placed, landed).astype(BF)
    unmix = same(landed, placed).astype(BF)

    leaving = select(blocks)
    arrived = lax.all_to_all(leaving.reshape(CHIPS, CHUNK, FIRST), ("x", "y"), 0, 0, tiled=True)
    mine = dot(sort, came.reshape(PARTS * QUARTER, PIECE)).astype(BF)
    mine = mine.reshape(PARTS, QUARTER, PIECE).transpose(1, 0, 2).reshape(QUARTER, SECOND)
    ahead = along(mine, 1)
    behind = along(mine, 3)
    top = along(ahead[:STRIP], 1)
    bottom = along(behind[STRIP:], 3)

    near = gate_up([mine, ahead, behind], w_gate, w_up)
    far = gate_up([top, bottom], w_gate, w_up)
    hidden = hidden_of(mix, arrived.reshape(ROWS, FIRST), w_gate, w_up, near, far)

    kept_rows, after, past_top, past_bottom, before = down_quarters(hidden, w_down)
    add_top = along(past_top, 3)
    add_bottom = along(past_bottom, 1)
    chunks = down_chunks(unmix, hidden, w_down)
    gathered = lax.all_to_all(chunks.reshape(CHIPS, CHUNK, FIRST), ("x", "y"), 0, 0, tiled=True)

    after = jnp.concatenate([(after[:STRIP].astype(F32) + add_top.astype(F32)).astype(BF), after[STRIP:]], axis=0)
    before = jnp.concatenate([before[:STRIP], (before[STRIP:].astype(F32) + add_bottom.astype(F32)).astype(BF)], axis=0)
    after = along(after, 3)
    before = along(before, 1)

    total = kept_rows.astype(F32) + after.astype(F32) + before.astype(F32)
    total = total.astype(BF).reshape(QUARTER, PARTS, PIECE).transpose(1, 0, 2)
    back = dot(unsort, total.reshape(PARTS * QUARTER, PIECE)).astype(BF)
    home = lax.all_to_all(back.reshape(EXPERTS, PARTS * SLOTS, PIECE), PLANE, 0, 0, tiled=True)

    kept, given = combine(gathered.reshape(ROWS, FIRST), blocks)
    taken = swap(given)
    both = (kept + taken.astype(F32)).reshape(4, TOK, FIRST)
    parts = []
    for step in (1, 3, 2):
        parts.append(along(both[step].astype(BF), 4 - step))
    return finish(home.reshape(SENT, PIECE), routes.T, scores.T, both[0], parts)


def solution(mesh):
    grid = Mesh(mesh.devices.reshape(4, 2, 4, 4), AXES)
    rows, blocks = P(AXES, None), P(AXES, None, None)
    return jax.shard_map(
        per_device,
        mesh=grid,
        in_specs=(rows, rows, rows, blocks, blocks, blocks),
        out_specs=rows,
        check_vma=False,
    )
```

time: 376 us -> 258 us (0.69)
  the two profiles are of different devices: /device:TPU:96 before, /device:TPU:6 now
where the time goes in v2:
time: 258 us; the launch traced here: 257 us
  waiting for transfers between devices  107 us (41%)
  Pallas kernels  70.4 us (27%)
  starting transfers between devices  53.7 us (21%)
  other arithmetic  10.1 us (4%)
  matrix products  8.66 us (3%)
  local copies, waits for them, and re-layouts  7.4 us (3%)
    ppermute x14, waiting for transfers between devices, along(): return lax.ppermute(x, 'z', [(i, (i + step) % 4) for i in range(4)])  54.3 us
    all_to_all x1, waiting for transfers between devices, per_device(): lax.all_to_all(chunks.reshape(CHIPS, CHUNK, FIRST), ('x', 'y'), 0, 0, til...  39.4 us
    ppermute x14, starting transfers between devices, along(): return lax.ppermute(x, 'z', [(i, (i + step) % 4) for i in range(4)])  23.3 us
    pallas_call x2, Pallas kernels, gate_up(): pl.pallas_call(functools.partial(gate_up_body, count), grid=(SECOND // TI...  16.2 us
    pallas_call x1, Pallas kernels, hidden_of(): pl.pallas_call(hidden_body, grid=(FIRST // TILE,), in_specs=[whole(HALF,...  12.2 us
    all_to_all x1, waiting for transfers between devices, per_device(): lax.all_to_all(back.reshape(EXPERTS, PARTS * SLOTS, PIECE), PLANE, 0, 0,...  11.3 us
    dot_general x2, matrix products, dot(): return jnp.dot(a, b, preferred_element_type=F32)  8.66 us
    pallas_call x1, Pallas kernels, select(): pl.pallas_call(select_body, grid=(FIRST // TILE,), in_specs=[column(TOK)]...  8.53 us
  transfers between devices with their start and end apart: 23, of which 10 were waited for; matrix products, arithmetic and copies ran while one was open for 9% of the time, Pallas kernels for 16%

profile of v2, /device:TPU:6, one launch (start us, length us, event | category | flops | bytes accessed | tf_op | source)
XLA Modules:
  0.0 257.4 jit_solution(16365861659208984723)
XLA Ops:
  0.0 5.3 %shard_map.64 = (bf16[64,3200]{1,0:T(8,128)(2,1)}, bf16[1280,512]{1,0:T(8,128)(2,1)}) custom-call(bf16[64,7168]{1,0:T(8,128)(2,1)} %tokens_ref.1, s32[2,64]{1,0:T(2,128)} %bitcast.47, f32[2,64]{1,0:T(2,128)} %bitcast.49), custom_call_target="tpu_custom_call" | custom-call | flops 671088640 | bytes 3000000 | tf_op jit(solution)/shard_map/pallas_call | solution.py:110
  5.3 7.8 %all-to-all-start.1 = ((bf16[32,40,512]{2,1,0:T(8,128)(2,1)}), bf16[32,40,512]{2,1,0:T(8,128)(2,1)}, u32[]{:S(2)}, u32[]{:S(2)}) async-start(bf16[32,40,512]{2,1,0:T(8,128)(2,1)} %bitcast.43), calls=%async_computation.1 | async-start | bytes 2621440 | tf_op jit(solution)/shard_map/all_to_all | solution.py:356
  13.1 2.0 collective-permute-start.1
  15.1 3.6 %collective-permute-start.3 = (bf16[64,3200]{1,0:T(8,128)(2,1)S(1)}, bf16[64,3200]{1,0:T(8,128)(2,1)S(1)}, u32[]{:S(2)}, u32[]{:S(2)}) collective-permute-start(bf16[64,3200]{1,0:T(8,128)(2,1)S(1)} %copy-done.4), channel_id=1, source_target_pairs={{0,2},{1,3},{2,0},{3,1},{4,6},{5,7},{6,4},{7,5},{8,10},{9,11},{10,... | collective-permute-start | bytes 1228808 | tf_op jit(solution)/shard_map/ppermute | solution.py:337
  19.7 7.3 %collective-permute-done.1.refs_2_.refs_10_ = bf16[64,3200]{1,0:T(8,128)(2,1)S(1)} collective-permute-done((bf16[64,3200]{1,0:T(8,128)(2,1)S(1)}, bf16[64,3200]{1,0:T(8,128)(2,1)S(1)}, u32[]{:S(2)}, u32[]{:S(2)}) %collective-permute-start.1) | collective-permute-done | bytes 409632 | tf_op jit(solution)/shard_map/ppermute | solution.py:337
  27.0 9.9 %collective-permute-done.3.refs_4_.refs_12_ = bf16[64,3200]{1,0:T(8,128)(2,1)S(1)} collective-permute-done((bf16[64,3200]{1,0:T(8,128)(2,1)S(1)}, bf16[64,3200]{1,0:T(8,128)(2,1)S(1)}, u32[]{:S(2)}, u32[]{:S(2)}) %collective-permute-start.3) | collective-permute-done | bytes 409632 | tf_op jit(solution)/shard_map/ppermute | solution.py:337
  40.2 8.5 %shard_map.65 = bf16[640,3072]{1,0:T(8,128)(2,1)} custom-call(bf16[64,3200]{1,0:T(8,128)(2,1)} %get-tuple-element.18.refs_0_.refs_8_, bf16[64,3200]{1,0:T(8,128)(2,1)} %copy-done.8, bf16[64,3200]{1,0:T(8,128)(2,1)} %copy-done.5, bf16[64,3200]{1,0:T(8,128)(2,1)} %copy-done.9, bf16[64,3200]{1,0:T(8,128)(2,1)} %copy-done.6, bf16[64,3200]{1,0:T(8,128)(2,1)} %copy-done.10, ...), custom_call_target="tpu_custom_call" | custom-call | flops 2013265920 | bytes 8000000 | tf_op jit(solution)/shard_map/pallas_call | solution.py:150
  48.8 7.2 %all-to-all-start = ((bf16[16,40,3072]{2,1,0:T(8,128)(2,1)}), bf16[16,40,3072]{2,1,0:T(8,128)(2,1)}, u32[]{:S(2)}, u32[]{:S(2)}) async-start(bf16[16,40,3072]{2,1,0:T(8,128)(2,1)} %bitcast.34), calls=%async_computation | async-start | bytes 7864320 | tf_op jit(solution)/shard_map/all_to_all | solution.py:378
  56.1 4.4 %fusion.43 = bf16[1280,512]{1,0:T(8,128)(2,1)S(1)} fusion(bf16[1280,512]{1,0:T(8,128)(2,1)} %bitcast.7, s32[1280]{0:T(1024)S(1)} %get-tuple-element.42, s32[1280]{0:T(1024)S(1)} %get-tuple-element.45, s32[1280]{0:T(1024)S(1)} %get-tuple-element.47, s32[1280]{0:T(1024)S(1)} %get-tuple-element.49, s32[1280]{0:T(1024)S(1)} %get-tuple-element.51, ...), kind=kOutput, calls=%fused_computation.42 | convolution fusion | flops 1693122560 | bytes 2672640 | tf_op jit(solution)/shard_map/dot_general | solution.py:38
  61.3 2.7 %collective-permute-start.8 = (bf16[160,4096]{1,0:T(8,128)(2,1)S(1)}, bf16[160,4096]{1,0:T(8,128)(2,1)S(1)}, u32[]{:S(2)}, u32[]{:S(2)}) collective-permute-start(bf16[160,4096]{1,0:T(8,128)(2,1)S(1)} %bitcast.39), channel_id=1, source_target_pairs={{0,3},{1,0},{2,1},{3,2},{4,7},{5,4},{6,5},{7,6},{8,11},{9,8},{10,9... | collective-permute-start | bytes 3932168 | tf_op jit(solution)/shard_map/ppermute | solution.py:337
  64.0 28.2 %collective-permute-done.7.refs_1_ = bf16[160,4096]{1,0:T(8,128)(2,1)S(1)} collective-permute-done((bf16[160,4096]{1,0:T(8,128)(2,1)S(1)}, bf16[160,4096]{1,0:T(8,128)(2,1)S(1)}, u32[]{:S(2)}, u32[]{:S(2)}) %collective-permute-start.7) | collective-permute-done | bytes 1310752 | tf_op jit(solution)/shard_map/ppermute | solution.py:337
  95.2 3.2 %collective-permute-start.10 = (bf16[80,4096]{1,0:T(8,128)(2,1)}, bf16[80,4096]{1,0:T(8,128)(2,1)}, u32[]{:S(2)}, u32[]{:S(2)}) collective-permute-start(bf16[80,4096]{1,0:T(8,128)(2,1)} %slice.48), channel_id=1, source_target_pairs={{0,3},{1,0},{2,1},{3,2},{4,7},{5,4},{6,5},{7,6},{8,11},{9,8},{10,9... | collective-permute-start | bytes 1966088 | tf_op jit(solution)/shard_map/ppermute | solution.py:337
  99.5 9.5 %shard_map.66 = (f32[480,512]{1,0:T(8,128)}, f32[480,512]{1,0:T(8,128)}) custom-call(bf16[160,4096]{1,0:T(8,128)(2,1)} %bitcast.40, bf16[160,4096]{1,0:T(8,128)(2,1)} %copy-done.2, bf16[160,4096]{1,0:T(8,128)(2,1)} %copy-done.3, bf16[7168,512]{1,0:T(8,128)(2,1)} %bitcast.28, bf16[7168,512]{1,0:T(8,128)(2,1)} %bitcast.31), custom_call_target="tpu_custom_call" | custom-call | flops 4026531840 | bytes 12000000 | tf_op jit(solution)/shard_map/pallas_call | solution.py:186
  110.1 1.3 collective-permute-done.10.refs_1_
  111.4 6.7 %shard_map.67 = (f32[160,512]{1,0:T(8,128)}, f32[160,512]{1,0:T(8,128)}) custom-call(bf16[80,4096]{1,0:T(8,128)(2,1)} %copy-done.14, bf16[80,4096]{1,0:T(8,128)(2,1)} %collective-permute-done.10.refs_1_, bf16[7168,512]{1,0:T(8,128)(2,1)} %bitcast.29, bf16[7168,512]{1,0:T(8,128)(2,1)} %bitcast.32), custom_call_target="tpu_custom_call" | custom-call | flops 1342177280 | bytes 12000000 | tf_op jit(solution)/shard_map/pallas_call | solution.py:186
  118.1 12.2 %shard_map.68.hidden_ref = bf16[640,512]{1,0:T(8,128)(2,1)} custom-call(bf16[320,320]{1,0:T(8,128)(2,1)} %get-tuple-element.37.mix_ref, bf16[640,3072]{1,0:T(8,128)(2,1)} %bitcast.3.rows_ref, bf16[7168,512]{1,0:T(8,128)(2,1)} %bitcast.30, bf16[7168,512]{1,0:T(8,128)(2,1)} %bitcast.33, f32[480,512]{1,0:T(8,128)} %get-tuple-element.20.gate_n, ...), custom_call_target="tpu_custom_call" | custom-call | flops 5284823040 | bytes 12000000 | tf_op jit(solution)/shard_map/pallas_call | solution.py:214
  130.3 8.5 %shard_map.69 = (bf16[160,4096]{1,0:T(8,128)(2,1)}, bf16[160,4096]{1,0:T(8,128)(2,1)}, bf16[80,4096]{1,0:T(8,128)(2,1)}, bf16[80,4096]{1,0:T(8,128)(2,1)}, bf16[160,4096]{1,0:T(8,128)(2,1)}) custom-call(bf16[640,512]{1,0:T(8,128)(2,1)} %shard_map.68.hidden_ref, bf16[512,7168]{1,0:T(8,128)(2,1)} %bitcast.36), custom_call_target="tpu_custom_call" | custom-call | flops 2684354560 | bytes 10000000 | tf_op jit(solution)/shard_map/pallas_call | solution.py:239
  140.3 3.8 %collective-permute-start.11 = (bf16[80,4096]{1,0:T(8,128)(2,1)}, bf16[80,4096]{1,0:T(8,128)(2,1)S(1)}, u32[]{:S(2)}, u32[]{:S(2)}) collective-permute-start(bf16[80,4096]{1,0:T(8,128)(2,1)} %get-tuple-element.26), channel_id=1, source_target_pairs={{0,3},{1,0},{2,1},{3,2},{4,7},{5,4},{6,5},{7,6},{8,11},{9,8},{10,9... | collective-permute-start | bytes 1966088 | tf_op jit(solution)/shard_map/ppermute | solution.py:337
  144.1 7.5 %shard_map.70 = bf16[640,3072]{1,0:T(8,128)(2,1)} custom-call(bf16[320,320]{1,0:T(8,128)(2,1)} %get-tuple-element.36.unmix_ref, bf16[640,512]{1,0:T(8,128)(2,1)} %shard_map.68.hidden_ref, bf16[512,7168]{1,0:T(8,128)(2,1)} %bitcast.37), custom_call_target="tpu_custom_call" | custom-call | flops 2013265920 | bytes 8000000 | tf_op jit(solution)/shard_map/pallas_call | solution.py:263
  151.6 7.1 %all-to-all-start.3 = ((bf16[16,40,3072]{2,1,0:T(8,128)(2,1)}), bf16[16,40,3072]{2,1,0:T(8,128)(2,1)}, u32[]{:S(2)}, u32[]{:S(2)}) async-start(bf16[16,40,3072]{2,1,0:T(8,128)(2,1)} %bitcast.35), calls=%async_computation.3 | async-start | bytes 7864320 | tf_op jit(solution)/shard_map/all_to_all | solution.py:394
  158.7 1.4 add_convert_fusion.1
  162.7 3.2 %collective-permute-start.12 = (bf16[160,4096]{1,0:T(8,128)(2,1)}, bf16[160,4096]{1,0:T(8,128)(2,1)}, u32[]{:S(2)}, u32[]{:S(2)}) collective-permute-start(bf16[160,4096]{1,0:T(8,128)(2,1)} %pad_maximum_fusion), channel_id=1, source_target_pairs={{0,3},{1,0},{2,1},{3,2},{4,7},{5,4},{6,5},{7,6},{8,11},{9,8},{10,9... | collective-permute-start | bytes 3932168 | tf_op jit(solution)/shard_map/ppermute | solution.py:337
  165.9 39.4 %all-to-all-done.3 = bf16[16,40,3072]{2,1,0:T(8,128)(2,1)} async-done(((bf16[16,40,3072]{2,1,0:T(8,128)(2,1)}), bf16[16,40,3072]{2,1,0:T(8,128)(2,1)}, u32[]{:S(2)}, u32[]{:S(2)}) %all-to-all-start.3) | async-done | bytes 3932192 | tf_op jit(solution)/shard_map/all_to_all | solution.py:394
  205.3 8.0 %shard_map.71 = (f32[256,3072]{1,0:T(8,128)}, bf16[256,3072]{1,0:T(8,128)(2,1)}) custom-call(bf16[640,3072]{1,0:T(8,128)(2,1)} %bitcast.16.rows_ref, bf16[64,3200]{1,0:T(8,128)(2,1)} %get-tuple-element.18.refs_0_.refs_8_, bf16[64,3200]{1,0:T(8,128)(2,1)} %copy-done.8, bf16[64,3200]{1,0:T(8,128)(2,1)} %copy-done.5, bf16[64,3200]{1,0:T(8,128)(2,1)} %copy-done.9, ...), custom_call_target="tpu_custom_call" | custom-call | flops 2013265920 | bytes 10000000 | tf_op jit(solution)/shard_map/pallas_call | solution.py:299
  213.3 2.3 add_convert_fusion
  215.8 4.2 %fusion.40 = bf16[1280,512]{1,0:T(8,128)(2,1)} fusion(bf16[1280,512]{1,0:T(8,128)(2,1)S(1)} %bitcast.45, s32[1280]{0:T(1024)S(1)} %get-tuple-element.43, s32[1280]{0:T(1024)S(1)} %get-tuple-element.44, s32[1280]{0:T(1024)S(1)} %get-tuple-element.46, s32[1280]{0:T(1024)S(1)} %get-tuple-element.48, s32[1280]{0:T(1024)S(1)} %get-tuple-element.50, ...), kind=kOutput, calls=%fused_computation.41 | convolution fusion | flops 1693122560 | bytes 2672640 | tf_op jit(solution)/shard_map/dot_general | solution.py:38
  220.0 7.9 %all-to-all-start.2 = ((bf16[32,40,512]{2,1,0:T(8,128)(2,1)}), bf16[32,40,512]{2,1,0:T(8,128)(2,1)S(1)}, u32[]{:S(2)}, u32[]{:S(2)}) async-start(bf16[32,40,512]{2,1,0:T(8,128)(2,1)} %bitcast.44), calls=%async_computation.2 | async-start | bytes 2621440 | tf_op jit(solution)/shard_map/all_to_all | solution.py:404
  227.9 2.5 fusion.95
  230.6 1.3 collective-permute-start.16
  234.6 11.3 %all-to-all-done.2 = bf16[32,40,512]{2,1,0:T(8,128)(2,1)S(1)} async-done(((bf16[32,40,512]{2,1,0:T(8,128)(2,1)}), bf16[32,40,512]{2,1,0:T(8,128)(2,1)S(1)}, u32[]{:S(2)}, u32[]{:S(2)}) %all-to-all-start.2) | async-done | bytes 1310752 | tf_op jit(solution)/shard_map/all_to_all | solution.py:404
  246.0 6.4 %collective-permute-done.17.b_ref = bf16[64,3072]{1,0:T(8,128)(2,1)S(1)} collective-permute-done((bf16[64,3072]{1,0:T(8,128)(2,1)S(1)}, bf16[64,3072]{1,0:T(8,128)(2,1)S(1)}, u32[]{:S(2)}, u32[]{:S(2)}) %collective-permute-start.17) | collective-permute-done | bytes 393248 | tf_op jit(solution)/shard_map/ppermute | solution.py:337
  253.1 4.3 %shard_map.72 = bf16[64,7168]{1,0:T(8,128)(2,1)} custom-call(bf16[1280,512]{1,0:T(8,128)(2,1)} %bitcast.42, s32[2,64]{1,0:T(2,128)} %bitcast.48, f32[2,64]{1,0:T(2,128)} %bitcast.50, f32[64,3072]{1,0:T(8,128)} %slice.49.kept, bf16[64,3072]{1,0:T(8,128)(2,1)} %copy-done.15, bf16[64,3072]{1,0:T(8,128)(2,1)} %copy-done.16, ...), custom_call_target="tpu_custom_call" | custom-call | flops 671088640 | bytes 5000000 | tf_op jit(solution)/shard_map/pallas_call | solution.py:328
  (82 shorter events, 18.0 us)
Async XLA Ops:
  5.3 7.8 %copy-start.4 = (bf16[64,3200]{1,0:T(8,128)(2,1)S(1)}, bf16[64,3200]{1,0:T(8,128)(2,1)}, u32[]{:S(2)}) copy-start(bf16[64,3200]{1,0:T(8,128)(2,1)} %get-tuple-element.18.refs_0_.refs_8_) | copy-start | bytes 1228804
  5.3 43.5 %all-to-all-start.1 = ((bf16[32,40,512]{2,1,0:T(8,128)(2,1)}), bf16[32,40,512]{2,1,0:T(8,128)(2,1)}, u32[]{:S(2)}, u32[]{:S(2)}) async-start(bf16[32,40,512]{2,1,0:T(8,128)(2,1)} %bitcast.43), calls=%async_computation.1 | async-start | bytes 2621440 | tf_op jit(solution)/shard_map/all_to_all | solution.py:356
  13.1 13.9 %collective-permute-start.1 = (bf16[64,3200]{1,0:T(8,128)(2,1)S(1)}, bf16[64,3200]{1,0:T(8,128)(2,1)S(1)}, u32[]{:S(2)}, u32[]{:S(2)}) collective-permute-start(bf16[64,3200]{1,0:T(8,128)(2,1)S(1)} %copy-done.4), channel_id=1, source_target_pairs={{0,1},{1,2},{2,3},{3,0},{4,5},{5,6},{6,7},{7,4},{8,9},{9,10},{10,1... | collective-permute-start | bytes 1228808 | tf_op jit(solution)/shard_map/ppermute | solution.py:337
  15.1 21.8 %collective-permute-start.3 = (bf16[64,3200]{1,0:T(8,128)(2,1)S(1)}, bf16[64,3200]{1,0:T(8,128)(2,1)S(1)}, u32[]{:S(2)}, u32[]{:S(2)}) collective-permute-start(bf16[64,3200]{1,0:T(8,128)(2,1)S(1)} %copy-done.4), channel_id=1, source_target_pairs={{0,2},{1,3},{2,0},{3,1},{4,6},{5,7},{6,4},{7,5},{8,10},{9,11},{10,... | collective-permute-start | bytes 1228808 | tf_op jit(solution)/shard_map/ppermute | solution.py:337
  18.7 18.3 %collective-permute-start.5 = (bf16[64,3200]{1,0:T(8,128)(2,1)S(1)}, bf16[64,3200]{1,0:T(8,128)(2,1)S(1)}, u32[]{:S(2)}, u32[]{:S(2)}) collective-permute-start(bf16[64,3200]{1,0:T(8,128)(2,1)S(1)} %copy-done.4), channel_id=1, source_target_pairs={{0,3},{1,0},{2,1},{3,2},{4,7},{5,4},{6,5},{7,6},{8,11},{9,8},{10,9... | collective-permute-start | bytes 1228808 | tf_op jit(solution)/shard_map/ppermute | solution.py:337
  19.7 17.8 %collective-permute-start = (bf16[64,3200]{1,0:T(8,128)(2,1)S(1)}, bf16[64,3200]{1,0:T(8,128)(2,1)S(1)}, u32[]{:S(2)}, u32[]{:S(2)}) collective-permute-start(bf16[64,3200]{1,0:T(8,128)(2,1)S(1)} %copy-done.4), channel_id=1, source_target_pairs={{0,16},{16,0},{1,17},{17,1},{2,18},{18,2},{3,19},{19,3},{4,20},{20... | collective-permute-start | bytes 1228808 | tf_op jit(solution)/shard_map/ppermute | solution.py:341
  27.0 12.3 %copy-start.5 = (bf16[64,3200]{1,0:T(8,128)(2,1)}, bf16[64,3200]{1,0:T(8,128)(2,1)S(1)}, u32[]{:S(2)}) copy-start(bf16[64,3200]{1,0:T(8,128)(2,1)S(1)} %collective-permute-done.1.refs_2_.refs_10_) | copy-start | bytes 1228804
  27.0 10.5 %collective-permute-start.2 = (bf16[64,3200]{1,0:T(8,128)(2,1)S(1)}, bf16[64,3200]{1,0:T(8,128)(2,1)S(1)}, u32[]{:S(2)}, u32[]{:S(2)}) collective-permute-start(bf16[64,3200]{1,0:T(8,128)(2,1)S(1)} %collective-permute-done.1.refs_2_.refs_10_), channel_id=1, source_target_pairs={{0,16},{16,0},{1,17},{17,1},{2,18},{18,2},{3,19},{19,3},{4,20},{20... | collective-permute-start | bytes 1228808 | tf_op jit(solution)/shard_map/ppermute | solution.py:341
  36.9 2.3 copy-start.6
  36.9 1.7 collective-permute-start.4
  36.9 2.3 copy-start.7
  37.0 2.3 collective-permute-start.6
  48.8 69.3 %all-to-all-start = ((bf16[16,40,3072]{2,1,0:T(8,128)(2,1)}), bf16[16,40,3072]{2,1,0:T(8,128)(2,1)}, u32[]{:S(2)}, u32[]{:S(2)}) async-start(bf16[16,40,3072]{2,1,0:T(8,128)(2,1)} %bitcast.34), calls=%async_computation | async-start | bytes 7864320 | tf_op jit(solution)/shard_map/all_to_all | solution.py:378
  60.7 38.8 %copy-start = (bf16[20,8,8,512]{3,1,2,0:T(8,128)(2,1)}, bf16[20,8,8,512]{3,1,2,0:T(8,128)(2,1)S(1)}, u32[]{:S(2)}) copy-start(bf16[20,8,8,512]{3,1,2,0:T(8,128)(2,1)S(1)} %copy.11) | copy-start | bytes 3932164
  60.7 31.5 %collective-permute-start.7 = (bf16[160,4096]{1,0:T(8,128)(2,1)S(1)}, bf16[160,4096]{1,0:T(8,128)(2,1)S(1)}, u32[]{:S(2)}, u32[]{:S(2)}) collective-permute-start(bf16[160,4096]{1,0:T(8,128)(2,1)S(1)} %bitcast.38), channel_id=1, source_target_pairs={{0,1},{1,2},{2,3},{3,0},{4,5},{5,6},{6,7},{7,4},{8,9},{9,10},{10,1... | collective-permute-start | bytes 3932168 | tf_op jit(solution)/shard_map/ppermute | solution.py:337
  61.3 31.9 %collective-permute-start.8 = (bf16[160,4096]{1,0:T(8,128)(2,1)S(1)}, bf16[160,4096]{1,0:T(8,128)(2,1)S(1)}, u32[]{:S(2)}, u32[]{:S(2)}) collective-permute-start(bf16[160,4096]{1,0:T(8,128)(2,1)S(1)} %bitcast.39), channel_id=1, source_target_pairs={{0,3},{1,0},{2,1},{3,2},{4,7},{5,4},{6,5},{7,6},{8,11},{9,8},{10,9... | collective-permute-start | bytes 3932168 | tf_op jit(solution)/shard_map/ppermute | solution.py:337
  92.2 7.3 %copy-start.2 = (bf16[160,4096]{1,0:T(8,128)(2,1)}, bf16[160,4096]{1,0:T(8,128)(2,1)S(1)}, u32[]{:S(2)}) copy-start(bf16[160,4096]{1,0:T(8,128)(2,1)S(1)} %collective-permute-done.7.refs_1_) | copy-start | bytes 3932164
  93.2 16.9 %collective-permute-start.9 = (bf16[80,4096]{1,0:T(8,128)(2,1)}, bf16[80,4096]{1,0:T(8,128)(2,1)S(1)}, u32[]{:S(2)}, u32[]{:S(2)}) collective-permute-start(bf16[80,4096]{1,0:T(8,128)(2,1)} %slice.47), channel_id=1, source_target_pairs={{0,1},{1,2},{2,3},{3,0},{4,5},{5,6},{6,7},{7,4},{8,9},{9,10},{10,1... | collective-permute-start | bytes 1966088 | tf_op jit(solution)/shard_map/ppermute | solution.py:337
  95.2 16.3 %collective-permute-start.10 = (bf16[80,4096]{1,0:T(8,128)(2,1)}, bf16[80,4096]{1,0:T(8,128)(2,1)}, u32[]{:S(2)}, u32[]{:S(2)}) collective-permute-start(bf16[80,4096]{1,0:T(8,128)(2,1)} %slice.48), channel_id=1, source_target_pairs={{0,3},{1,0},{2,1},{3,2},{4,7},{5,4},{6,5},{7,6},{8,11},{9,8},{10,9... | collective-permute-start | bytes 1966088 | tf_op jit(solution)/shard_map/ppermute | solution.py:337
  138.7 20.0 %collective-permute-start.13 = (bf16[80,4096]{1,0:T(8,128)(2,1)}, bf16[80,4096]{1,0:T(8,128)(2,1)}, u32[]{:S(2)}, u32[]{:S(2)}) collective-permute-start(bf16[80,4096]{1,0:T(8,128)(2,1)} %get-tuple-element.28), channel_id=1, source_target_pairs={{0,1},{1,2},{2,3},{3,0},{4,5},{5,6},{6,7},{7,4},{8,9},{9,10},{10,1... | collective-permute-start | bytes 1966088 | tf_op jit(solution)/shard_map/ppermute | solution.py:337
  140.3 21.0 %collective-permute-start.11 = (bf16[80,4096]{1,0:T(8,128)(2,1)}, bf16[80,4096]{1,0:T(8,128)(2,1)S(1)}, u32[]{:S(2)}, u32[]{:S(2)}) collective-permute-start(bf16[80,4096]{1,0:T(8,128)(2,1)} %get-tuple-element.26), channel_id=1, source_target_pairs={{0,3},{1,0},{2,1},{3,2},{4,7},{5,4},{6,5},{7,6},{8,11},{9,8},{10,9... | collective-permute-start | bytes 1966088 | tf_op jit(solution)/shard_map/ppermute | solution.py:337
  151.6 53.7 %all-to-all-start.3 = ((bf16[16,40,3072]{2,1,0:T(8,128)(2,1)}), bf16[16,40,3072]{2,1,0:T(8,128)(2,1)}, u32[]{:S(2)}, u32[]{:S(2)}) async-start(bf16[16,40,3072]{2,1,0:T(8,128)(2,1)} %bitcast.35), calls=%async_computation.3 | async-start | bytes 7864320 | tf_op jit(solution)/shard_map/all_to_all | solution.py:394
  161.3 52.0 %collective-permute-start.14 = (bf16[160,4096]{1,0:T(8,128)(2,1)}, bf16[160,4096]{1,0:T(8,128)(2,1)}, u32[]{:S(2)}, u32[]{:S(2)}) collective-permute-start(bf16[160,4096]{1,0:T(8,128)(2,1)} %pad_maximum_fusion.1), channel_id=1, source_target_pairs={{0,1},{1,2},{2,3},{3,0},{4,5},{5,6},{6,7},{7,4},{8,9},{9,10},{10,1... | collective-permute-start | bytes 3932168 | tf_op jit(solution)/shard_map/ppermute | solution.py:337
  162.7 50.6 %collective-permute-start.12 = (bf16[160,4096]{1,0:T(8,128)(2,1)}, bf16[160,4096]{1,0:T(8,128)(2,1)}, u32[]{:S(2)}, u32[]{:S(2)}) collective-permute-start(bf16[160,4096]{1,0:T(8,128)(2,1)} %pad_maximum_fusion), channel_id=1, source_target_pairs={{0,3},{1,0},{2,1},{3,2},{4,7},{5,4},{6,5},{7,6},{8,11},{9,8},{10,9... | collective-permute-start | bytes 3932168 | tf_op jit(solution)/shard_map/ppermute | solution.py:337
  205.3 8.0 %copy-start.12 = (bf16[160,4096]{1,0:T(8,128)(2,1)S(1)}, bf16[160,4096]{1,0:T(8,128)(2,1)}, u32[]{:S(2)}) copy-start(bf16[160,4096]{1,0:T(8,128)(2,1)} %get-tuple-element.24) | copy-start | bytes 3932164
  213.3 14.6 %collective-permute-start.15 = (bf16[256,3072]{1,0:T(8,128)(2,1)}, bf16[256,3072]{1,0:T(8,128)(2,1)S(1)}, u32[]{:S(2)}, u32[]{:S(2)}) collective-permute-start(bf16[256,3072]{1,0:T(8,128)(2,1)} %get-tuple-element.30), channel_id=1, source_target_pairs={{0,16},{16,0},{1,17},{17,1},{2,18},{18,2},{3,19},{19,3},{4,20},{20... | collective-permute-start | bytes 4718600 | tf_op jit(solution)/shard_map/ppermute | solution.py:341
  220.0 25.9 %all-to-all-start.2 = ((bf16[32,40,512]{2,1,0:T(8,128)(2,1)}), bf16[32,40,512]{2,1,0:T(8,128)(2,1)S(1)}, u32[]{:S(2)}, u32[]{:S(2)}) async-start(bf16[32,40,512]{2,1,0:T(8,128)(2,1)} %bitcast.44), calls=%async_computation.2 | async-start | bytes 2621440 | tf_op jit(solution)/shard_map/all_to_all | solution.py:404
  230.6 15.4 %collective-permute-start.16 = (bf16[64,3072]{1,0:T(8,128)(2,1)S(1)}, bf16[64,3072]{1,0:T(8,128)(2,1)S(1)}, u32[]{:S(2)}, u32[]{:S(2)}) collective-permute-start(bf16[64,3072]{1,0:T(8,128)(2,1)S(1)} %get-tuple-element.35), channel_id=1, source_target_pairs={{0,3},{1,0},{2,1},{3,2},{4,7},{5,4},{6,5},{7,6},{8,11},{9,8},{10,9... | collective-permute-start | bytes 1179656 | tf_op jit(solution)/shard_map/ppermute | solution.py:337
  231.8 20.5 %collective-permute-start.17 = (bf16[64,3072]{1,0:T(8,128)(2,1)S(1)}, bf16[64,3072]{1,0:T(8,128)(2,1)S(1)}, u32[]{:S(2)}, u32[]{:S(2)}) collective-permute-start(bf16[64,3072]{1,0:T(8,128)(2,1)S(1)} %get-tuple-element.34), channel_id=1, source_target_pairs={{0,1},{1,2},{2,3},{3,0},{4,5},{5,6},{6,7},{7,4},{8,9},{9,10},{10,1... | collective-permute-start | bytes 1179656 | tf_op jit(solution)/shard_map/ppermute | solution.py:337
  232.7 19.7 %collective-permute-start.18 = (bf16[64,3072]{1,0:T(8,128)(2,1)S(1)}, bf16[64,3072]{1,0:T(8,128)(2,1)}, u32[]{:S(2)}, u32[]{:S(2)}) collective-permute-start(bf16[64,3072]{1,0:T(8,128)(2,1)S(1)} %get-tuple-element.33), channel_id=1, source_target_pairs={{0,2},{1,3},{2,0},{3,1},{4,6},{5,7},{6,4},{7,5},{8,10},{9,11},{10,... | collective-permute-start | bytes 1179656 | tf_op jit(solution)/shard_map/ppermute | solution.py:337
  246.0 6.4 %copy-start.1 = (bf16[32,40,512]{2,1,0:T(8,128)(2,1)}, bf16[32,40,512]{2,1,0:T(8,128)(2,1)S(1)}, u32[]{:S(2)}) copy-start(bf16[32,40,512]{2,1,0:T(8,128)(2,1)S(1)} %all-to-all-done.2) | copy-start | bytes 3932164
  246.0 6.4 %copy-start.15 = (bf16[64,3072]{1,0:T(8,128)(2,1)}, bf16[64,3072]{1,0:T(8,128)(2,1)S(1)}, u32[]{:S(2)}) copy-start(bf16[64,3072]{1,0:T(8,128)(2,1)S(1)} %collective-permute-done.16.a_ref) | copy-start | bytes 1179652
  (8 other events, 9.9 us)

commit v3 on v2

--- a/solution.py
+++ b/solution.py
@@ -31,7 +31,7 @@
 HALF = ROWS // 2
 FACTS = 128
 TILE = 1024
-STEP = 256
+STEP = 1024
 
 
 def dot(a, b):
@@ -51,11 +51,8 @@
 
 
 def each(width, step, body):
-    def run(i, carry):
-        body(pl.ds(pl.multiple_of(i * step, step), step))
-        return carry
-
-    lax.fori_loop(0, width // step, run, 0)
+    for at in range(0, width, step):
+        body(slice(at, at + step))
 
 
 def iota(shape, axis):
@@ -103,7 +100,7 @@
     def body(rows):
         send_ref[rows, :] = dot(pick_ref[rows, :], stacked).astype(BF)
 
-    each(SENT, 320, body)
+    each(SENT, SENT, body)
 
 
 def send(tokens, routes, scores):
@@ -168,7 +165,7 @@
         gate[:, cols] += dot(rows, gate_w[:, cols])
         up[:, cols] += dot(rows, up_w[:, cols])
 
-    each(HID, STEP, body)
+    each(HID, HID, body)
 
 
 def gate_up_body(count, *refs):
@@ -193,7 +190,7 @@
     )(*blocks, gate_w, up_w)
 
 
-def hidden_body(mix_ref, rows_ref, gate_w, up_w, gate_n, up_n, gate_f, up_f, out, gate, up):
+def hidden_body(mix_ref, rows_ref, gate_w, up_w, gate_o, up_o, gate_n, up_n, gate_f, up_f, out, gate, up):
     rows = [dot(mix_ref[...], rows_ref[h * HALF:(h + 1) * HALF]).astype(BF) for h in range(2)]
     accumulate(jnp.concatenate(rows, axis=0), gate_w, up_w, gate, up)
 
@@ -202,25 +199,24 @@
         for k in range(4):
             for h in range(2):
                 at, mixed = k * QUARTER + h * STRIP, h * HALF + k * STRIP
-                place = (0, 1, None, 2)[k]
-                g_ref, u_ref = (gate_f, up_f) if place is None else (gate_n, up_n)
-                off = h * STRIP + (place or 0) * QUARTER
+                g_ref, u_ref = ((gate_o, up_o), (gate_n, up_n), (gate_f, up_f), (gate_n, up_n))[k]
+                off = h * STRIP + (QUARTER if k == 3 else 0)
                 g = gate[mixed:mixed + STRIP] + g_ref[off:off + STRIP]
                 u = up[mixed:mixed + STRIP] + u_ref[off:off + STRIP]
                 out[at:at + STRIP] = (g / (1.0 + jnp.exp(-g)) * u).astype(BF)
 
 
-def hidden_of(mix, rows, gate_w, up_w, near, far):
+def hidden_of(mix, rows, gate_w, up_w, alone, near, far):
     return pl.pallas_call(
         hidden_body,
         grid=(FIRST // TILE,),
         in_specs=[whole(HALF, HALF), column(ROWS)] + [weight_tile(0)] * 2
-        + [whole(3 * QUARTER, HID)] * 2 + [whole(QUARTER, HID)] * 2,
+        + [whole(QUARTER, HID)] * 2 + [whole(2 * QUARTER, HID)] * 2 + [whole(QUARTER, HID)] * 2,
         out_specs=whole(ROWS, HID),
         out_shape=jax.ShapeDtypeStruct((ROWS, HID), BF),
         scratch_shapes=[pltpu.VMEM((ROWS, HID), F32)] * 2,
         cost_estimate=cost(2 * ROWS * FIRST * (2 * HID + HALF), 12_000_000),
-    )(mix, rows, gate_w, up_w, *near, *far)
+    )(mix, rows, gate_w, up_w, *alone, *near, *far)
 
 
 SPANS = ((0, QUARTER), (QUARTER, QUARTER), (2 * QUARTER, STRIP), (2 * QUARTER + STRIP, STRIP), (3 * QUARTER, QUARTER))
@@ -383,9 +379,10 @@
     top = along(ahead[:STRIP], 1)
     bottom = along(behind[STRIP:], 3)
 
-    near = gate_up([mine, ahead, behind], w_gate, w_up)
+    alone = gate_up([mine], w_gate, w_up)
+    near = gate_up([ahead, behind], w_gate, w_up)
     far = gate_up([top, bottom], w_gate, w_up)
-    hidden = hidden_of(mix, arrived.reshape(ROWS, FIRST), w_gate, w_up, near, far)
+    hidden = hidden_of(mix, arrived.reshape(ROWS, FIRST), w_gate, w_up, alone, near, far)
 
     kept_rows, after, past_top, past_bottom, before = down_quarters(hidden, w_down)
     add_top = along(past_top, 3)

time: 258 us -> 249 us (0.965)
  the two profiles are of different devices: /device:TPU:6 before, /device:TPU:96 now
where the time goes in v3:
time: 249 us; the launch traced here: 244 us
  waiting for transfers between devices  107 us (43%)
  Pallas kernels  66.7 us (27%)
  starting transfers between devices  46.4 us (19%)
  other arithmetic  8.8 us (4%)
  matrix products  8.67 us (3%)
  local copies, waits for them, and re-layouts  5.96 us (2%)
    ppermute x14, waiting for transfers between devices, along(): return lax.ppermute(x, 'z', [(i, (i + step) % 4) for i in range(4)])  63.3 us
    all_to_all x1, waiting for transfers between devices, per_device(): lax.all_to_all(chunks.reshape(CHIPS, CHUNK, FIRST), ('x', 'y'), 0, 0, til...  30.4 us
    ppermute x14, starting transfers between devices, along(): return lax.ppermute(x, 'z', [(i, (i + step) % 4) for i in range(4)])  20.5 us
    pallas_call x3, Pallas kernels, gate_up(): pl.pallas_call(functools.partial(gate_up_body, count), grid=(SECOND // TI...  19.5 us
    all_to_all x1, waiting for transfers between devices, per_device(): lax.all_to_all(back.reshape(EXPERTS, PARTS * SLOTS, PIECE), PLANE, 0, 0,...  11.8 us
    pallas_call x1, Pallas kernels, hidden_of(): pl.pallas_call(hidden_body, grid=(FIRST // TILE,), in_specs=[whole(HALF,...  11.8 us
    dot_general x2, matrix products, dot(): return jnp.dot(a, b, preferred_element_type=F32)  8.67 us
    all_to_all x1, starting transfers between devices, per_device(): lax.all_to_all(sending.reshape(EXPERTS, PARTS * SLOTS, PIECE), PLANE, 0,...  7.56 us
  transfers between devices with their start and end apart: 23, of which 10 were waited for; matrix products, arithmetic and copies ran while one was open for 8% of the time, Pallas kernels for 16%

profile of v3, /device:TPU:96, one launch (start us, length us, event | category | flops | bytes accessed | tf_op | source)
XLA Modules:
  0.0 244.2 jit_solution(16750659243390342881)
XLA Ops:
  0.0 3.8 %shard_map.64 = (bf16[64,3200]{1,0:T(8,128)(2,1)}, bf16[1280,512]{1,0:T(8,128)(2,1)}) custom-call(bf16[64,7168]{1,0:T(8,128)(2,1)} %tokens_ref.1, s32[2,64]{1,0:T(2,128)} %bitcast.49, f32[2,64]{1,0:T(2,128)} %bitcast.51), custom_call_target="tpu_custom_call" | custom-call | flops 671088640 | bytes 3000000 | tf_op jit(solution)/shard_map/pallas_call | solution.py:107
  3.8 7.6 %all-to-all-start.1 = ((bf16[32,40,512]{2,1,0:T(8,128)(2,1)}), bf16[32,40,512]{2,1,0:T(8,128)(2,1)}, u32[]{:S(2)}, u32[]{:S(2)}) async-start(bf16[32,40,512]{2,1,0:T(8,128)(2,1)} %bitcast.45), calls=%async_computation.1 | async-start | bytes 2621440 | tf_op jit(solution)/shard_map/all_to_all | solution.py:352
  11.5 2.5 %collective-permute-start.3 = (bf16[64,3200]{1,0:T(8,128)(2,1)S(1)}, bf16[64,3200]{1,0:T(8,128)(2,1)S(1)}, u32[]{:S(2)}, u32[]{:S(2)}) collective-permute-start(bf16[64,3200]{1,0:T(8,128)(2,1)S(1)} %copy-done.4), channel_id=1, source_target_pairs={{0,2},{1,3},{2,0},{3,1},{4,6},{5,7},{6,4},{7,5},{8,10},{9,11},{10,... | collective-permute-start | bytes 1228808 | tf_op jit(solution)/shard_map/ppermute | solution.py:333
  14.0 9.9 %collective-permute-done.1.refs_2_.refs_10_ = bf16[64,3200]{1,0:T(8,128)(2,1)S(1)} collective-permute-done((bf16[64,3200]{1,0:T(8,128)(2,1)S(1)}, bf16[64,3200]{1,0:T(8,128)(2,1)S(1)}, u32[]{:S(2)}, u32[]{:S(2)}) %collective-permute-start.1) | collective-permute-done | bytes 409632 | tf_op jit(solution)/shard_map/ppermute | solution.py:333
  25.5 8.0 %collective-permute-done.5.refs_6_.refs_14_ = bf16[64,3200]{1,0:T(8,128)(2,1)S(1)} collective-permute-done((bf16[64,3200]{1,0:T(8,128)(2,1)S(1)}, bf16[64,3200]{1,0:T(8,128)(2,1)S(1)}, u32[]{:S(2)}, u32[]{:S(2)}) %collective-permute-start.5) | collective-permute-done | bytes 409632 | tf_op jit(solution)/shard_map/ppermute | solution.py:333
  36.0 7.4 %shard_map.65 = bf16[640,3072]{1,0:T(8,128)(2,1)} custom-call(bf16[64,3200]{1,0:T(8,128)(2,1)} %get-tuple-element.20.refs_0_.refs_8_, bf16[64,3200]{1,0:T(8,128)(2,1)} %copy-done.8, bf16[64,3200]{1,0:T(8,128)(2,1)} %copy-done.5, bf16[64,3200]{1,0:T(8,128)(2,1)} %copy-done.9, bf16[64,3200]{1,0:T(8,128)(2,1)} %copy-done.6, bf16[64,3200]{1,0:T(8,128)(2,1)} %copy-done.10, ...), custom_call_target="tpu_custom_call" | custom-call | flops 2013265920 | bytes 8000000 | tf_op jit(solution)/shard_map/pallas_call | solution.py:147
  43.4 7.0 %all-to-all-start = ((bf16[16,40,3072]{2,1,0:T(8,128)(2,1)}), bf16[16,40,3072]{2,1,0:T(8,128)(2,1)}, u32[]{:S(2)}, u32[]{:S(2)}) async-start(bf16[16,40,3072]{2,1,0:T(8,128)(2,1)} %bitcast.36), calls=%async_computation | async-start | bytes 7864320 | tf_op jit(solution)/shard_map/all_to_all | solution.py:374
  50.6 4.4 %fusion.43 = bf16[1280,512]{1,0:T(8,128)(2,1)S(1)} fusion(bf16[1280,512]{1,0:T(8,128)(2,1)} %bitcast.7, s32[1280]{0:T(1024)S(1)} %get-tuple-element.46, s32[1280]{0:T(1024)S(1)} %get-tuple-element.49, s32[1280]{0:T(1024)S(1)} %get-tuple-element.51, s32[1280]{0:T(1024)S(1)} %get-tuple-element.53, s32[1280]{0:T(1024)S(1)} %get-tuple-element.55, ...), kind=kOutput, calls=%fused_computation.42 | convolution fusion | flops 1693122560 | bytes 2672640 | tf_op jit(solution)/shard_map/dot_general | solution.py:38
  55.9 2.6 %collective-permute-start.7 = (bf16[160,4096]{1,0:T(8,128)(2,1)S(1)}, bf16[160,4096]{1,0:T(8,128)(2,1)S(1)}, u32[]{:S(2)}, u32[]{:S(2)}) collective-permute-start(bf16[160,4096]{1,0:T(8,128)(2,1)S(1)} %bitcast.43), channel_id=1, source_target_pairs={{0,1},{1,2},{2,3},{3,0},{4,5},{5,6},{6,7},{7,4},{8,9},{9,10},{10,1... | collective-permute-start | bytes 3932168 | tf_op jit(solution)/shard_map/ppermute | solution.py:333
  58.5 28.5 %collective-permute-done.8.refs_1_ = bf16[160,4096]{1,0:T(8,128)(2,1)S(1)} collective-permute-done((bf16[160,4096]{1,0:T(8,128)(2,1)S(1)}, bf16[160,4096]{1,0:T(8,128)(2,1)S(1)}, u32[]{:S(2)}, u32[]{:S(2)}) %collective-permute-start.8) | collective-permute-done | bytes 1310752 | tf_op jit(solution)/shard_map/ppermute | solution.py:333
  89.9 3.2 %collective-permute-start.9 = (bf16[80,4096]{1,0:T(8,128)(2,1)}, bf16[80,4096]{1,0:T(8,128)(2,1)}, u32[]{:S(2)}, u32[]{:S(2)}) collective-permute-start(bf16[80,4096]{1,0:T(8,128)(2,1)} %slice.47), channel_id=1, source_target_pairs={{0,1},{1,2},{2,3},{3,0},{4,5},{5,6},{6,7},{7,4},{8,9},{9,10},{10,1... | collective-permute-start | bytes 1966088 | tf_op jit(solution)/shard_map/ppermute | solution.py:333
  94.2 6.0 %shard_map.66 = (f32[160,512]{1,0:T(8,128)}, f32[160,512]{1,0:T(8,128)}) custom-call(bf16[160,4096]{1,0:T(8,128)(2,1)} %bitcast.44, bf16[7168,512]{1,0:T(8,128)(2,1)} %bitcast.28, bf16[7168,512]{1,0:T(8,128)(2,1)} %bitcast.32), custom_call_target="tpu_custom_call" | custom-call | flops 1342177280 | bytes 12000000 | tf_op jit(solution)/shard_map/pallas_call | solution.py:183
  100.3 7.3 %shard_map.67 = (f32[320,512]{1,0:T(8,128)}, f32[320,512]{1,0:T(8,128)}) custom-call(bf16[160,4096]{1,0:T(8,128)(2,1)} %copy-done.3, bf16[160,4096]{1,0:T(8,128)(2,1)} %copy-done.2, bf16[7168,512]{1,0:T(8,128)(2,1)} %bitcast.29, bf16[7168,512]{1,0:T(8,128)(2,1)} %bitcast.33), custom_call_target="tpu_custom_call" | custom-call | flops 2684354560 | bytes 12000000 | tf_op jit(solution)/shard_map/pallas_call | solution.py:183
  108.5 6.1 %shard_map.68 = (f32[160,512]{1,0:T(8,128)}, f32[160,512]{1,0:T(8,128)}) custom-call(bf16[80,4096]{1,0:T(8,128)(2,1)} %collective-permute-done.9.refs_0_, bf16[80,4096]{1,0:T(8,128)(2,1)} %copy-done.15, bf16[7168,512]{1,0:T(8,128)(2,1)} %bitcast.30, bf16[7168,512]{1,0:T(8,128)(2,1)} %bitcast.34), custom_call_target="tpu_custom_call" | custom-call | flops 1342177280 | bytes 12000000 | tf_op jit(solution)/shard_map/pallas_call | solution.py:183
  114.6 11.8 %shard_map.69.hidden_ref = bf16[640,512]{1,0:T(8,128)(2,1)} custom-call(bf16[320,320]{1,0:T(8,128)(2,1)} %get-tuple-element.41.mix_ref, bf16[640,3072]{1,0:T(8,128)(2,1)} %bitcast.3.rows_ref, bf16[7168,512]{1,0:T(8,128)(2,1)} %bitcast.31, bf16[7168,512]{1,0:T(8,128)(2,1)} %bitcast.35, f32[160,512]{1,0:T(8,128)} %get-tuple-element.22.gate_o, ...), custom_call_target="tpu_custom_call" | custom-call | flops 5284823040 | bytes 12000000 | tf_op jit(solution)/shard_map/pallas_call | solution.py:210
  126.4 6.7 %shard_map.70 = (bf16[160,4096]{1,0:T(8,128)(2,1)}, bf16[160,4096]{1,0:T(8,128)(2,1)}, bf16[80,4096]{1,0:T(8,128)(2,1)}, bf16[80,4096]{1,0:T(8,128)(2,1)}, bf16[160,4096]{1,0:T(8,128)(2,1)}) custom-call(bf16[640,512]{1,0:T(8,128)(2,1)} %shard_map.69.hidden_ref, bf16[512,7168]{1,0:T(8,128)(2,1)} %bitcast.38), custom_call_target="tpu_custom_call" | custom-call | flops 2684354560 | bytes 10000000 | tf_op jit(solution)/shard_map/pallas_call | solution.py:235
  133.1 6.5 %shard_map.71 = bf16[640,3072]{1,0:T(8,128)(2,1)} custom-call(bf16[320,320]{1,0:T(8,128)(2,1)} %get-tuple-element.40.unmix_ref, bf16[640,512]{1,0:T(8,128)(2,1)} %shard_map.69.hidden_ref, bf16[512,7168]{1,0:T(8,128)(2,1)} %bitcast.39), custom_call_target="tpu_custom_call" | custom-call | flops 2013265920 | bytes 8000000 | tf_op jit(solution)/shard_map/pallas_call | solution.py:259
  139.6 7.1 %all-to-all-start.3 = ((bf16[16,40,3072]{2,1,0:T(8,128)(2,1)}), bf16[16,40,3072]{2,1,0:T(8,128)(2,1)}, u32[]{:S(2)}, u32[]{:S(2)}) async-start(bf16[16,40,3072]{2,1,0:T(8,128)(2,1)} %bitcast.37), calls=%async_computation.3 | async-start | bytes 7864320 | tf_op jit(solution)/shard_map/all_to_all | solution.py:391
  146.7 3.3 %collective-permute-start.13 = (bf16[80,4096]{1,0:T(8,128)(2,1)S(1)}, bf16[80,4096]{1,0:T(8,128)(2,1)S(1)}, u32[]{:S(2)}, u32[]{:S(2)}) collective-permute-start(bf16[80,4096]{1,0:T(8,128)(2,1)S(1)} %copy-done.18), channel_id=1, source_target_pairs={{0,1},{1,2},{2,3},{3,0},{4,5},{5,6},{6,7},{7,4},{8,9},{9,10},{10,1... | collective-permute-start | bytes 1966088 | tf_op jit(solution)/shard_map/ppermute | solution.py:333
  151.4 10.4 %collective-permute-done.13 = bf16[80,4096]{1,0:T(8,128)(2,1)S(1)} collective-permute-done((bf16[80,4096]{1,0:T(8,128)(2,1)S(1)}, bf16[80,4096]{1,0:T(8,128)(2,1)S(1)}, u32[]{:S(2)}, u32[]{:S(2)}) %collective-permute-start.13) | collective-permute-done | bytes 655392 | tf_op jit(solution)/shard_map/ppermute | solution.py:333
  163.1 3.7 %collective-permute-start.14 = (bf16[160,4096]{1,0:T(8,128)(2,1)}, bf16[160,4096]{1,0:T(8,128)(2,1)}, u32[]{:S(2)}, u32[]{:S(2)}) collective-permute-start(bf16[160,4096]{1,0:T(8,128)(2,1)} %pad_maximum_fusion.1), channel_id=1, source_target_pairs={{0,1},{1,2},{2,3},{3,0},{4,5},{5,6},{6,7},{7,4},{8,9},{9,10},{10,1... | collective-permute-start | bytes 3932168 | tf_op jit(solution)/shard_map/ppermute | solution.py:333
  166.8 30.4 %all-to-all-done.3 = bf16[16,40,3072]{2,1,0:T(8,128)(2,1)} async-done(((bf16[16,40,3072]{2,1,0:T(8,128)(2,1)}), bf16[16,40,3072]{2,1,0:T(8,128)(2,1)}, u32[]{:S(2)}, u32[]{:S(2)}) %all-to-all-start.3) | async-done | bytes 3932192 | tf_op jit(solution)/shard_map/all_to_all | solution.py:391
  197.2 6.8 %shard_map.72 = (f32[256,3072]{1,0:T(8,128)}, bf16[256,3072]{1,0:T(8,128)(2,1)}) custom-call(bf16[640,3072]{1,0:T(8,128)(2,1)} %bitcast.16.rows_ref, bf16[64,3200]{1,0:T(8,128)(2,1)} %get-tuple-element.20.refs_0_.refs_8_, bf16[64,3200]{1,0:T(8,128)(2,1)} %copy-done.8, bf16[64,3200]{1,0:T(8,128)(2,1)} %copy-done.5, bf16[64,3200]{1,0:T(8,128)(2,1)} %copy-done.9, ...), custom_call_target="tpu_custom_call" | custom-call | flops 2013265920 | bytes 10000000 | tf_op jit(solution)/shard_map/pallas_call | solution.py:295
  204.0 2.3 add_convert_fusion
  206.5 4.3 %fusion.40 = bf16[1280,512]{1,0:T(8,128)(2,1)} fusion(bf16[1280,512]{1,0:T(8,128)(2,1)S(1)} %bitcast.47, s32[1280]{0:T(1024)S(1)} %get-tuple-element.47, s32[1280]{0:T(1024)S(1)} %get-tuple-element.48, s32[1280]{0:T(1024)S(1)} %get-tuple-element.50, s32[1280]{0:T(1024)S(1)} %get-tuple-element.52, s32[1280]{0:T(1024)S(1)} %get-tuple-element.54, ...), kind=kOutput, calls=%fused_computation.41 | convolution fusion | flops 1693122560 | bytes 2672640 | tf_op jit(solution)/shard_map/dot_general | solution.py:38
  210.7 4.3 %all-to-all-start.2 = ((bf16[32,40,512]{2,1,0:T(8,128)(2,1)}), bf16[32,40,512]{2,1,0:T(8,128)(2,1)S(1)}, u32[]{:S(2)}, u32[]{:S(2)}) async-start(bf16[32,40,512]{2,1,0:T(8,128)(2,1)} %bitcast.46), calls=%async_computation.2 | async-start | bytes 2621440 | tf_op jit(solution)/shard_map/all_to_all | solution.py:401
  215.1 2.5 %fusion.95 = (bf16[256,3072]{1,0:T(8,128)(2,1)S(1)}, f32[256,3072]{1,0:T(8,128)S(1)}) fusion(f32[256,3072]{1,0:T(8,128)} %get-tuple-element.33, bf16[256,3072]{1,0:T(8,128)(2,1)S(1)} %collective-permute-done.15), kind=kLoop, calls=%fused_computation.153 | loop fusion | flops 2359296 | bytes 9437184 | tf_op jit(solution)/shard_map/convert.2
  218.6 2.4 collective-permute-start.17
  223.1 11.8 %all-to-all-done.2 = bf16[32,40,512]{2,1,0:T(8,128)(2,1)S(1)} async-done(((bf16[32,40,512]{2,1,0:T(8,128)(2,1)}), bf16[32,40,512]{2,1,0:T(8,128)(2,1)S(1)}, u32[]{:S(2)}, u32[]{:S(2)}) %all-to-all-start.2) | async-done | bytes 1310752 | tf_op jit(solution)/shard_map/all_to_all | solution.py:401
  234.9 3.1 %collective-permute-done.17.b_ref = bf16[64,3072]{1,0:T(8,128)(2,1)S(1)} collective-permute-done((bf16[64,3072]{1,0:T(8,128)(2,1)S(1)}, bf16[64,3072]{1,0:T(8,128)(2,1)S(1)}, u32[]{:S(2)}, u32[]{:S(2)}) %collective-permute-start.17) | collective-permute-done | bytes 393248 | tf_op jit(solution)/shard_map/ppermute | solution.py:333
  238.0 1.9 collective-permute-done.18.c_ref
  239.9 4.3 %shard_map.73 = bf16[64,7168]{1,0:T(8,128)(2,1)} custom-call(bf16[1280,512]{1,0:T(8,128)(2,1)} %bitcast.41, s32[2,64]{1,0:T(2,128)} %bitcast.50, f32[2,64]{1,0:T(2,128)} %bitcast.52, f32[64,3072]{1,0:T(8,128)} %slice.49.kept, bf16[64,3072]{1,0:T(8,128)(2,1)} %copy-done.16, bf16[64,3072]{1,0:T(8,128)(2,1)} %copy-done.17, ...), custom_call_target="tpu_custom_call" | custom-call | flops 671088640 | bytes 5000000 | tf_op jit(solution)/shard_map/pallas_call | solution.py:324
  (87 shorter events, 16.1 us)
Async XLA Ops:
  3.8 7.6 %copy-start.4 = (bf16[64,3200]{1,0:T(8,128)(2,1)S(1)}, bf16[64,3200]{1,0:T(8,128)(2,1)}, u32[]{:S(2)}) copy-start(bf16[64,3200]{1,0:T(8,128)(2,1)} %get-tuple-element.20.refs_0_.refs_8_) | copy-start | bytes 1228804
  3.8 39.6 %all-to-all-start.1 = ((bf16[32,40,512]{2,1,0:T(8,128)(2,1)}), bf16[32,40,512]{2,1,0:T(8,128)(2,1)}, u32[]{:S(2)}, u32[]{:S(2)}) async-start(bf16[32,40,512]{2,1,0:T(8,128)(2,1)} %bitcast.45), calls=%async_computation.1 | async-start | bytes 2621440 | tf_op jit(solution)/shard_map/all_to_all | solution.py:352
  11.4 12.4 %collective-permute-start.1 = (bf16[64,3200]{1,0:T(8,128)(2,1)S(1)}, bf16[64,3200]{1,0:T(8,128)(2,1)S(1)}, u32[]{:S(2)}, u32[]{:S(2)}) collective-permute-start(bf16[64,3200]{1,0:T(8,128)(2,1)S(1)} %copy-done.4), channel_id=1, source_target_pairs={{0,1},{1,2},{2,3},{3,0},{4,5},{5,6},{6,7},{7,4},{8,9},{9,10},{10,1... | collective-permute-start | bytes 1228808 | tf_op jit(solution)/shard_map/ppermute | solution.py:333
  11.5 14.0 %collective-permute-start.3 = (bf16[64,3200]{1,0:T(8,128)(2,1)S(1)}, bf16[64,3200]{1,0:T(8,128)(2,1)S(1)}, u32[]{:S(2)}, u32[]{:S(2)}) collective-permute-start(bf16[64,3200]{1,0:T(8,128)(2,1)S(1)} %copy-done.4), channel_id=1, source_target_pairs={{0,2},{1,3},{2,0},{3,1},{4,6},{5,7},{6,4},{7,5},{8,10},{9,11},{10,... | collective-permute-start | bytes 1228808 | tf_op jit(solution)/shard_map/ppermute | solution.py:333
  14.0 19.5 %collective-permute-start.5 = (bf16[64,3200]{1,0:T(8,128)(2,1)S(1)}, bf16[64,3200]{1,0:T(8,128)(2,1)S(1)}, u32[]{:S(2)}, u32[]{:S(2)}) collective-permute-start(bf16[64,3200]{1,0:T(8,128)(2,1)S(1)} %copy-done.4), channel_id=1, source_target_pairs={{0,3},{1,0},{2,1},{3,2},{4,7},{5,4},{6,5},{7,6},{8,11},{9,8},{10,9... | collective-permute-start | bytes 1228808 | tf_op jit(solution)/shard_map/ppermute | solution.py:333
  14.0 19.5 %collective-permute-start = (bf16[64,3200]{1,0:T(8,128)(2,1)S(1)}, bf16[64,3200]{1,0:T(8,128)(2,1)S(1)}, u32[]{:S(2)}, u32[]{:S(2)}) collective-permute-start(bf16[64,3200]{1,0:T(8,128)(2,1)S(1)} %copy-done.4), channel_id=1, source_target_pairs={{0,16},{16,0},{1,17},{17,1},{2,18},{18,2},{3,19},{19,3},{4,20},{20... | collective-permute-start | bytes 1228808 | tf_op jit(solution)/shard_map/ppermute | solution.py:337
  23.8 11.4 %copy-start.5 = (bf16[64,3200]{1,0:T(8,128)(2,1)}, bf16[64,3200]{1,0:T(8,128)(2,1)S(1)}, u32[]{:S(2)}) copy-start(bf16[64,3200]{1,0:T(8,128)(2,1)S(1)} %collective-permute-done.1.refs_2_.refs_10_) | copy-start | bytes 1228804
  23.8 9.6 %collective-permute-start.2 = (bf16[64,3200]{1,0:T(8,128)(2,1)S(1)}, bf16[64,3200]{1,0:T(8,128)(2,1)S(1)}, u32[]{:S(2)}, u32[]{:S(2)}) collective-permute-start(bf16[64,3200]{1,0:T(8,128)(2,1)S(1)} %collective-permute-done.1.refs_2_.refs_10_), channel_id=1, source_target_pairs={{0,16},{16,0},{1,17},{17,1},{2,18},{18,2},{3,19},{19,3},{4,20},{20... | collective-permute-start | bytes 1228808 | tf_op jit(solution)/shard_map/ppermute | solution.py:337
  25.5 9.7 %copy-start.6 = (bf16[64,3200]{1,0:T(8,128)(2,1)}, bf16[64,3200]{1,0:T(8,128)(2,1)S(1)}, u32[]{:S(2)}) copy-start(bf16[64,3200]{1,0:T(8,128)(2,1)S(1)} %collective-permute-done.3.refs_4_.refs_12_) | copy-start | bytes 1228804
  25.5 8.0 %collective-permute-start.4 = (bf16[64,3200]{1,0:T(8,128)(2,1)S(1)}, bf16[64,3200]{1,0:T(8,128)(2,1)S(1)}, u32[]{:S(2)}, u32[]{:S(2)}) collective-permute-start(bf16[64,3200]{1,0:T(8,128)(2,1)S(1)} %collective-permute-done.3.refs_4_.refs_12_), channel_id=1, source_target_pairs={{0,16},{16,0},{1,17},{17,1},{2,18},{18,2},{3,19},{19,3},{4,20},{20... | collective-permute-start | bytes 1228808 | tf_op jit(solution)/shard_map/ppermute | solution.py:337
  33.4 1.7 collective-permute-start.6
  43.4 71.2 %all-to-all-start = ((bf16[16,40,3072]{2,1,0:T(8,128)(2,1)}), bf16[16,40,3072]{2,1,0:T(8,128)(2,1)}, u32[]{:S(2)}, u32[]{:S(2)}) async-start(bf16[16,40,3072]{2,1,0:T(8,128)(2,1)} %bitcast.36), calls=%async_computation | async-start | bytes 7864320 | tf_op jit(solution)/shard_map/all_to_all | solution.py:374
  55.1 39.1 %copy-start.1 = (bf16[20,8,8,512]{3,1,2,0:T(8,128)(2,1)}, bf16[20,8,8,512]{3,1,2,0:T(8,128)(2,1)S(1)}, u32[]{:S(2)}) copy-start(bf16[20,8,8,512]{3,1,2,0:T(8,128)(2,1)S(1)} %copy.11) | copy-start | bytes 3932164
  55.2 31.8 %collective-permute-start.8 = (bf16[160,4096]{1,0:T(8,128)(2,1)S(1)}, bf16[160,4096]{1,0:T(8,128)(2,1)S(1)}, u32[]{:S(2)}, u32[]{:S(2)}) collective-permute-start(bf16[160,4096]{1,0:T(8,128)(2,1)S(1)} %bitcast.42), channel_id=1, source_target_pairs={{0,3},{1,0},{2,1},{3,2},{4,7},{5,4},{6,5},{7,6},{8,11},{9,8},{10,9... | collective-permute-start | bytes 3932168 | tf_op jit(solution)/shard_map/ppermute | solution.py:333
  55.9 32.1 %collective-permute-start.7 = (bf16[160,4096]{1,0:T(8,128)(2,1)S(1)}, bf16[160,4096]{1,0:T(8,128)(2,1)S(1)}, u32[]{:S(2)}, u32[]{:S(2)}) collective-permute-start(bf16[160,4096]{1,0:T(8,128)(2,1)S(1)} %bitcast.43), channel_id=1, source_target_pairs={{0,1},{1,2},{2,3},{3,0},{4,5},{5,6},{6,7},{7,4},{8,9},{9,10},{10,1... | collective-permute-start | bytes 3932168 | tf_op jit(solution)/shard_map/ppermute | solution.py:333
  87.0 13.3 %copy-start.2 = (bf16[160,4096]{1,0:T(8,128)(2,1)}, bf16[160,4096]{1,0:T(8,128)(2,1)S(1)}, u32[]{:S(2)}) copy-start(bf16[160,4096]{1,0:T(8,128)(2,1)S(1)} %collective-permute-done.8.refs_1_) | copy-start | bytes 3932164
  87.9 19.7 %collective-permute-start.10 = (bf16[80,4096]{1,0:T(8,128)(2,1)}, bf16[80,4096]{1,0:T(8,128)(2,1)S(1)}, u32[]{:S(2)}, u32[]{:S(2)}) collective-permute-start(bf16[80,4096]{1,0:T(8,128)(2,1)} %slice.48), channel_id=1, source_target_pairs={{0,3},{1,0},{2,1},{3,2},{4,7},{5,4},{6,5},{7,6},{8,11},{9,8},{10,9... | collective-permute-start | bytes 1966088 | tf_op jit(solution)/shard_map/ppermute | solution.py:333
  89.9 17.7 %collective-permute-start.9 = (bf16[80,4096]{1,0:T(8,128)(2,1)}, bf16[80,4096]{1,0:T(8,128)(2,1)}, u32[]{:S(2)}, u32[]{:S(2)}) collective-permute-start(bf16[80,4096]{1,0:T(8,128)(2,1)} %slice.47), channel_id=1, source_target_pairs={{0,1},{1,2},{2,3},{3,0},{4,5},{5,6},{6,7},{7,4},{8,9},{9,10},{10,1... | collective-permute-start | bytes 1966088 | tf_op jit(solution)/shard_map/ppermute | solution.py:333
  133.1 17.0 %collective-permute-start.11 = (bf16[80,4096]{1,0:T(8,128)(2,1)}, bf16[80,4096]{1,0:T(8,128)(2,1)S(1)}, u32[]{:S(2)}, u32[]{:S(2)}) collective-permute-start(bf16[80,4096]{1,0:T(8,128)(2,1)} %get-tuple-element.30), channel_id=1, source_target_pairs={{0,3},{1,0},{2,1},{3,2},{4,7},{5,4},{6,5},{7,6},{8,11},{9,8},{10,9... | collective-permute-start | bytes 1966088 | tf_op jit(solution)/shard_map/ppermute | solution.py:333
  139.6 7.1 %copy-start.14 = (bf16[160,4096]{1,0:T(8,128)(2,1)S(1)}, bf16[160,4096]{1,0:T(8,128)(2,1)}, u32[]{:S(2)}) copy-start(bf16[160,4096]{1,0:T(8,128)(2,1)} %get-tuple-element.29) | copy-start | bytes 3932164
  139.6 7.2 %copy-start.18 = (bf16[80,4096]{1,0:T(8,128)(2,1)S(1)}, bf16[80,4096]{1,0:T(8,128)(2,1)}, u32[]{:S(2)}) copy-start(bf16[80,4096]{1,0:T(8,128)(2,1)} %get-tuple-element.32) | copy-start | bytes 1966084
  139.6 57.6 %all-to-all-start.3 = ((bf16[16,40,3072]{2,1,0:T(8,128)(2,1)}), bf16[16,40,3072]{2,1,0:T(8,128)(2,1)}, u32[]{:S(2)}, u32[]{:S(2)}) async-start(bf16[16,40,3072]{2,1,0:T(8,128)(2,1)} %bitcast.37), calls=%async_computation.3 | async-start | bytes 7864320 | tf_op jit(solution)/shard_map/all_to_all | solution.py:391
  146.7 15.0 %collective-permute-start.13 = (bf16[80,4096]{1,0:T(8,128)(2,1)S(1)}, bf16[80,4096]{1,0:T(8,128)(2,1)S(1)}, u32[]{:S(2)}, u32[]{:S(2)}) collective-permute-start(bf16[80,4096]{1,0:T(8,128)(2,1)S(1)} %copy-done.18), channel_id=1, source_target_pairs={{0,1},{1,2},{2,3},{3,0},{4,5},{5,6},{6,7},{7,4},{8,9},{9,10},{10,1... | collective-permute-start | bytes 1966088 | tf_op jit(solution)/shard_map/ppermute | solution.py:333
  151.4 52.6 %collective-permute-start.12 = (bf16[160,4096]{1,0:T(8,128)(2,1)}, bf16[160,4096]{1,0:T(8,128)(2,1)}, u32[]{:S(2)}, u32[]{:S(2)}) collective-permute-start(bf16[160,4096]{1,0:T(8,128)(2,1)} %pad_maximum_fusion), channel_id=1, source_target_pairs={{0,3},{1,0},{2,1},{3,2},{4,7},{5,4},{6,5},{7,6},{8,11},{9,8},{10,9... | collective-permute-start | bytes 3932168 | tf_op jit(solution)/shard_map/ppermute | solution.py:333
  163.1 40.9 %collective-permute-start.14 = (bf16[160,4096]{1,0:T(8,128)(2,1)}, bf16[160,4096]{1,0:T(8,128)(2,1)}, u32[]{:S(2)}, u32[]{:S(2)}) collective-permute-start(bf16[160,4096]{1,0:T(8,128)(2,1)} %pad_maximum_fusion.1), channel_id=1, source_target_pairs={{0,1},{1,2},{2,3},{3,0},{4,5},{5,6},{6,7},{7,4},{8,9},{9,10},{10,1... | collective-permute-start | bytes 3932168 | tf_op jit(solution)/shard_map/ppermute | solution.py:333
  197.2 6.8 %copy-start.12 = (bf16[160,4096]{1,0:T(8,128)(2,1)S(1)}, bf16[160,4096]{1,0:T(8,128)(2,1)}, u32[]{:S(2)}) copy-start(bf16[160,4096]{1,0:T(8,128)(2,1)} %get-tuple-element.28) | copy-start | bytes 3932164
  204.0 11.1 %collective-permute-start.15 = (bf16[256,3072]{1,0:T(8,128)(2,1)}, bf16[256,3072]{1,0:T(8,128)(2,1)S(1)}, u32[]{:S(2)}, u32[]{:S(2)}) collective-permute-start(bf16[256,3072]{1,0:T(8,128)(2,1)} %get-tuple-element.34), channel_id=1, source_target_pairs={{0,16},{16,0},{1,17},{17,1},{2,18},{18,2},{3,19},{19,3},{4,20},{20... | collective-permute-start | bytes 4718600 | tf_op jit(solution)/shard_map/ppermute | solution.py:337
  210.7 24.2 %all-to-all-start.2 = ((bf16[32,40,512]{2,1,0:T(8,128)(2,1)}), bf16[32,40,512]{2,1,0:T(8,128)(2,1)S(1)}, u32[]{:S(2)}, u32[]{:S(2)}) async-start(bf16[32,40,512]{2,1,0:T(8,128)(2,1)} %bitcast.46), calls=%async_computation.2 | async-start | bytes 2621440 | tf_op jit(solution)/shard_map/all_to_all | solution.py:401
  217.7 17.2 %collective-permute-start.16 = (bf16[64,3072]{1,0:T(8,128)(2,1)S(1)}, bf16[64,3072]{1,0:T(8,128)(2,1)S(1)}, u32[]{:S(2)}, u32[]{:S(2)}) collective-permute-start(bf16[64,3072]{1,0:T(8,128)(2,1)S(1)} %get-tuple-element.39), channel_id=1, source_target_pairs={{0,3},{1,0},{2,1},{3,2},{4,7},{5,4},{6,5},{7,6},{8,11},{9,8},{10,9... | collective-permute-start | bytes 1179656 | tf_op jit(solution)/shard_map/ppermute | solution.py:333
  218.6 19.4 %collective-permute-start.17 = (bf16[64,3072]{1,0:T(8,128)(2,1)S(1)}, bf16[64,3072]{1,0:T(8,128)(2,1)S(1)}, u32[]{:S(2)}, u32[]{:S(2)}) collective-permute-start(bf16[64,3072]{1,0:T(8,128)(2,1)S(1)} %get-tuple-element.38), channel_id=1, source_target_pairs={{0,1},{1,2},{2,3},{3,0},{4,5},{5,6},{6,7},{7,4},{8,9},{9,10},{10,1... | collective-permute-start | bytes 1179656 | tf_op jit(solution)/shard_map/ppermute | solution.py:333
  221.0 18.9 %collective-permute-start.18 = (bf16[64,3072]{1,0:T(8,128)(2,1)S(1)}, bf16[64,3072]{1,0:T(8,128)(2,1)}, u32[]{:S(2)}, u32[]{:S(2)}) collective-permute-start(bf16[64,3072]{1,0:T(8,128)(2,1)S(1)} %get-tuple-element.37), channel_id=1, source_target_pairs={{0,2},{1,3},{2,0},{3,1},{4,6},{5,7},{6,4},{7,5},{8,10},{9,11},{10,... | collective-permute-start | bytes 1179656 | tf_op jit(solution)/shard_map/ppermute | solution.py:333
  234.9 5.0 %copy-start = (bf16[32,40,512]{2,1,0:T(8,128)(2,1)}, bf16[32,40,512]{2,1,0:T(8,128)(2,1)S(1)}, u32[]{:S(2)}) copy-start(bf16[32,40,512]{2,1,0:T(8,128)(2,1)S(1)} %all-to-all-done.2) | copy-start | bytes 3932164
  (10 other events, 20.0 us)

commit v4 on v3

--- a/solution.py
+++ b/solution.py
@@ -219,26 +219,28 @@
     )(mix, rows, gate_w, up_w, *alone, *near, *far)
 
 
-SPANS = ((0, QUARTER), (QUARTER, QUARTER), (2 * QUARTER, STRIP), (2 * QUARTER + STRIP, STRIP), (3 * QUARTER, QUARTER))
-
-
-def down_quarters_body(hidden_ref, w_ref, *outs):
-    def body(cols):
-        rows = dot(hidden_ref[...], w_ref[:, cols]).astype(BF)
-        for (at, size), out in zip(SPANS, outs):
-            out[:, cols] = rows[at:at + size]
-
-    each(TILE, STEP, body)
-
-
-def down_quarters(hidden, w_down):
-    return pl.pallas_call(
-        down_quarters_body,
+NEAR_SPANS = ((0, QUARTER), (QUARTER, QUARTER), (3 * QUARTER, QUARTER))
+FAR_SPANS = ((2 * QUARTER, STRIP), (2 * QUARTER + STRIP, STRIP))
+
+
+def down_quarters_body(spans, hidden_ref, w_ref, *outs):
+    hidden = jnp.concatenate([hidden_ref[at:at + size] for at, size in spans], axis=0)
+    rows = dot(hidden, w_ref[...]).astype(BF)
+    done = 0
+    for (_, size), out in zip(spans, outs):
+        out[...] = rows[done:done + size]
+        done += size
+
+
+def down_quarters(spans, hidden, w_down):
+    rows = sum(size for _, size in spans)
+    return pl.pallas_call(
+        functools.partial(down_quarters_body, spans),
         grid=(SECOND // TILE,),
         in_specs=[whole(ROWS, HID), column(HID, skip=FIRST // TILE)],
-        out_specs=[column(size) for _, size in SPANS],
-        out_shape=[jax.ShapeDtypeStruct((size, SECOND), BF) for _, size in SPANS],
-        cost_estimate=cost(2 * ROWS * HID * SECOND, 10_000_000),
+        out_specs=[column(size) for _, size in spans],
+        out_shape=[jax.ShapeDtypeStruct((size, SECOND), BF) for _, size in spans],
+        cost_estimate=cost(2 * rows * HID * SECOND, 8_000_000),
     )(hidden, w_down)
 
 
@@ -384,12 +386,13 @@
     far = gate_up([top, bottom], w_gate, w_up)
     hidden = hidden_of(mix, arrived.reshape(ROWS, FIRST), w_gate, w_up, alone, near, far)
 
-    kept_rows, after, past_top, past_bottom, before = down_quarters(hidden, w_down)
+    past_top, past_bottom = down_quarters(FAR_SPANS, hidden, w_down)
     add_top = along(past_top, 3)
     add_bottom = along(past_bottom, 1)
     chunks = down_chunks(unmix, hidden, w_down)
     gathered = lax.all_to_all(chunks.reshape(CHIPS, CHUNK, FIRST), ("x", "y"), 0, 0, tiled=True)
 
+    kept_rows, after, before = down_quarters(NEAR_SPANS, hidden, w_down)
     after = jnp.concatenate([(after[:STRIP].astype(F32) + add_top.astype(F32)).astype(BF), after[STRIP:]], axis=0)
     before = jnp.concatenate([before[:STRIP], (before[STRIP:].astype(F32) + add_bottom.astype(F32)).astype(BF)], axis=0)
     after = along(after, 3)

time: 249 us -> 247 us (level)
  waiting for transfers between devices: 107 us -> 100 us
  Pallas kernels: 66.7 us -> 71.2 us
    all_to_all x1, waiting for transfers between devices: 30.4 us -> 23.1 us  [per_device(): lax.all_to_all(chunks.reshape(CHIPS, CHUNK, FIRST), ('x', 'y'), 0, 0, til...]
    pallas_call x1 -> x2, Pallas kernels: 6.68 us -> 10.9 us  [down_quarters(): pl.pallas_call(functools.partial(down_quarters_body, spans), grid=(SECOND...]
  transfers between devices with their start and end apart: 23 -> 23, of which waited for: 10 -> 10; matrix products, arithmetic and copies ran while one was open for 8% -> 9% of each run, Pallas kernels for 16% -> 19%
where the time goes in v4:
time: 247 us; the launch traced here: 243 us
  waiting for transfers between devices  100 us (40%)
  Pallas kernels  71.2 us (29%)
  starting transfers between devices  46.3 us (19%)
  other arithmetic  8.83 us (4%)
  matrix products  8.66 us (4%)
  local copies, waits for them, and re-layouts  7.25 us (3%)
    ppermute x14, waiting for transfers between devices, along(): return lax.ppermute(x, 'z', [(i, (i + step) % 4) for i in range(4)])  63.3 us
    all_to_all x1, waiting for transfers between devices, per_device(): lax.all_to_all(chunks.reshape(CHIPS, CHUNK, FIRST), ('x', 'y'), 0, 0, til...  23.1 us
    ppermute x14, starting transfers between devices, along(): return lax.ppermute(x, 'z', [(i, (i + step) % 4) for i in range(4)])  20.5 us
    pallas_call x3, Pallas kernels, gate_up(): pl.pallas_call(functools.partial(gate_up_body, count), grid=(SECOND // TI...  19.5 us
    all_to_all x1, waiting for transfers between devices, per_device(): lax.all_to_all(back.reshape(EXPERTS, PARTS * SLOTS, PIECE), PLANE, 0, 0,...  11.8 us
    pallas_call x1, Pallas kernels, hidden_of(): pl.pallas_call(hidden_body, grid=(FIRST // TILE,), in_specs=[whole(HALF,...  11.7 us
    pallas_call x2, Pallas kernels, down_quarters(): pl.pallas_call(functools.partial(down_quarters_body, spans), grid=(SECOND...  10.9 us
    dot_general x2, matrix products, dot(): return jnp.dot(a, b, preferred_element_type=F32)  8.66 us
  transfers between devices with their start and end apart: 23, of which 10 were waited for; matrix products, arithmetic and copies ran while one was open for 9% of the time, Pallas kernels for 19%

profile of v4, /device:TPU:96, one launch (start us, length us, event | category | flops | bytes accessed | tf_op | source)
XLA Modules:
  0.0 242.6 jit_solution(14231535719538759749)
XLA Ops:
  0.0 3.8 %shard_map.64 = (bf16[64,3200]{1,0:T(8,128)(2,1)}, bf16[1280,512]{1,0:T(8,128)(2,1)}) custom-call(bf16[64,7168]{1,0:T(8,128)(2,1)} %tokens_ref.1, s32[2,64]{1,0:T(2,128)} %bitcast.50, f32[2,64]{1,0:T(2,128)} %bitcast.52), custom_call_target="tpu_custom_call" | custom-call | flops 671088640 | bytes 3000000 | tf_op jit(solution)/shard_map/pallas_call | solution.py:107
  3.8 7.6 %all-to-all-start.1 = ((bf16[32,40,512]{2,1,0:T(8,128)(2,1)}), bf16[32,40,512]{2,1,0:T(8,128)(2,1)}, u32[]{:S(2)}, u32[]{:S(2)}) async-start(bf16[32,40,512]{2,1,0:T(8,128)(2,1)} %bitcast.46), calls=%async_computation.1 | async-start | bytes 2621440 | tf_op jit(solution)/shard_map/all_to_all | solution.py:354
  11.5 2.5 %collective-permute-start.3 = (bf16[64,3200]{1,0:T(8,128)(2,1)S(1)}, bf16[64,3200]{1,0:T(8,128)(2,1)S(1)}, u32[]{:S(2)}, u32[]{:S(2)}) collective-permute-start(bf16[64,3200]{1,0:T(8,128)(2,1)S(1)} %copy-done.4), channel_id=1, source_target_pairs={{0,2},{1,3},{2,0},{3,1},{4,6},{5,7},{6,4},{7,5},{8,10},{9,11},{10,... | collective-permute-start | bytes 1228808 | tf_op jit(solution)/shard_map/ppermute | solution.py:335
  14.0 9.9 %collective-permute-done.1.refs_2_.refs_10_ = bf16[64,3200]{1,0:T(8,128)(2,1)S(1)} collective-permute-done((bf16[64,3200]{1,0:T(8,128)(2,1)S(1)}, bf16[64,3200]{1,0:T(8,128)(2,1)S(1)}, u32[]{:S(2)}, u32[]{:S(2)}) %collective-permute-start.1) | collective-permute-done | bytes 409632 | tf_op jit(solution)/shard_map/ppermute | solution.py:335
  25.5 8.0 %collective-permute-done.5.refs_6_.refs_14_ = bf16[64,3200]{1,0:T(8,128)(2,1)S(1)} collective-permute-done((bf16[64,3200]{1,0:T(8,128)(2,1)S(1)}, bf16[64,3200]{1,0:T(8,128)(2,1)S(1)}, u32[]{:S(2)}, u32[]{:S(2)}) %collective-permute-start.5) | collective-permute-done | bytes 409632 | tf_op jit(solution)/shard_map/ppermute | solution.py:335
  36.0 7.5 %shard_map.65 = bf16[640,3072]{1,0:T(8,128)(2,1)} custom-call(bf16[64,3200]{1,0:T(8,128)(2,1)} %get-tuple-element.20.refs_0_.refs_8_, bf16[64,3200]{1,0:T(8,128)(2,1)} %copy-done.8, bf16[64,3200]{1,0:T(8,128)(2,1)} %copy-done.5, bf16[64,3200]{1,0:T(8,128)(2,1)} %copy-done.9, bf16[64,3200]{1,0:T(8,128)(2,1)} %copy-done.6, bf16[64,3200]{1,0:T(8,128)(2,1)} %copy-done.10, ...), custom_call_target="tpu_custom_call" | custom-call | flops 2013265920 | bytes 8000000 | tf_op jit(solution)/shard_map/pallas_call | solution.py:147
  43.5 7.0 %all-to-all-start = ((bf16[16,40,3072]{2,1,0:T(8,128)(2,1)}), bf16[16,40,3072]{2,1,0:T(8,128)(2,1)}, u32[]{:S(2)}, u32[]{:S(2)}) async-start(bf16[16,40,3072]{2,1,0:T(8,128)(2,1)} %bitcast.39), calls=%async_computation | async-start | bytes 7864320 | tf_op jit(solution)/shard_map/all_to_all | solution.py:376
  50.7 4.4 %fusion.43 = bf16[1280,512]{1,0:T(8,128)(2,1)S(1)} fusion(bf16[1280,512]{1,0:T(8,128)(2,1)} %bitcast.7, s32[1280]{0:T(1024)S(1)} %get-tuple-element.46, s32[1280]{0:T(1024)S(1)} %get-tuple-element.49, s32[1280]{0:T(1024)S(1)} %get-tuple-element.51, s32[1280]{0:T(1024)S(1)} %get-tuple-element.53, s32[1280]{0:T(1024)S(1)} %get-tuple-element.55, ...), kind=kOutput, calls=%fused_computation.42 | convolution fusion | flops 1693122560 | bytes 2672640 | tf_op jit(solution)/shard_map/dot_general | solution.py:38
  56.0 2.6 %collective-permute-start.7 = (bf16[160,4096]{1,0:T(8,128)(2,1)S(1)}, bf16[160,4096]{1,0:T(8,128)(2,1)S(1)}, u32[]{:S(2)}, u32[]{:S(2)}) collective-permute-start(bf16[160,4096]{1,0:T(8,128)(2,1)S(1)} %bitcast.44), channel_id=1, source_target_pairs={{0,1},{1,2},{2,3},{3,0},{4,5},{5,6},{6,7},{7,4},{8,9},{9,10},{10,1... | collective-permute-start | bytes 3932168 | tf_op jit(solution)/shard_map/ppermute | solution.py:335
  58.6 28.5 %collective-permute-done.8.refs_1_ = bf16[160,4096]{1,0:T(8,128)(2,1)S(1)} collective-permute-done((bf16[160,4096]{1,0:T(8,128)(2,1)S(1)}, bf16[160,4096]{1,0:T(8,128)(2,1)S(1)}, u32[]{:S(2)}, u32[]{:S(2)}) %collective-permute-start.8) | collective-permute-done | bytes 1310752 | tf_op jit(solution)/shard_map/ppermute | solution.py:335
  90.0 3.2 %collective-permute-start.9 = (bf16[80,4096]{1,0:T(8,128)(2,1)}, bf16[80,4096]{1,0:T(8,128)(2,1)}, u32[]{:S(2)}, u32[]{:S(2)}) collective-permute-start(bf16[80,4096]{1,0:T(8,128)(2,1)} %slice.47), channel_id=1, source_target_pairs={{0,1},{1,2},{2,3},{3,0},{4,5},{5,6},{6,7},{7,4},{8,9},{9,10},{10,1... | collective-permute-start | bytes 1966088 | tf_op jit(solution)/shard_map/ppermute | solution.py:335
  94.4 6.0 %shard_map.66 = (f32[160,512]{1,0:T(8,128)}, f32[160,512]{1,0:T(8,128)}) custom-call(bf16[160,4096]{1,0:T(8,128)(2,1)} %bitcast.45, bf16[7168,512]{1,0:T(8,128)(2,1)} %bitcast.28, bf16[7168,512]{1,0:T(8,128)(2,1)} %bitcast.32), custom_call_target="tpu_custom_call" | custom-call | flops 1342177280 | bytes 12000000 | tf_op jit(solution)/shard_map/pallas_call | solution.py:183
  100.4 7.3 %shard_map.67 = (f32[320,512]{1,0:T(8,128)}, f32[320,512]{1,0:T(8,128)}) custom-call(bf16[160,4096]{1,0:T(8,128)(2,1)} %copy-done.3, bf16[160,4096]{1,0:T(8,128)(2,1)} %copy-done.2, bf16[7168,512]{1,0:T(8,128)(2,1)} %bitcast.29, bf16[7168,512]{1,0:T(8,128)(2,1)} %bitcast.33), custom_call_target="tpu_custom_call" | custom-call | flops 2684354560 | bytes 12000000 | tf_op jit(solution)/shard_map/pallas_call | solution.py:183
  108.7 6.1 %shard_map.68 = (f32[160,512]{1,0:T(8,128)}, f32[160,512]{1,0:T(8,128)}) custom-call(bf16[80,4096]{1,0:T(8,128)(2,1)} %collective-permute-done.9.refs_0_, bf16[80,4096]{1,0:T(8,128)(2,1)} %copy-done.15, bf16[7168,512]{1,0:T(8,128)(2,1)} %bitcast.30, bf16[7168,512]{1,0:T(8,128)(2,1)} %bitcast.34), custom_call_target="tpu_custom_call" | custom-call | flops 1342177280 | bytes 12000000 | tf_op jit(solution)/shard_map/pallas_call | solution.py:183
  114.8 11.7 %shard_map.69.hidden_ref = bf16[640,512]{1,0:T(8,128)(2,1)} custom-call(bf16[320,320]{1,0:T(8,128)(2,1)} %get-tuple-element.41.mix_ref, bf16[640,3072]{1,0:T(8,128)(2,1)} %bitcast.3.rows_ref, bf16[7168,512]{1,0:T(8,128)(2,1)} %bitcast.31, bf16[7168,512]{1,0:T(8,128)(2,1)} %bitcast.35, f32[160,512]{1,0:T(8,128)} %get-tuple-element.22.gate_o, ...), custom_call_target="tpu_custom_call" | custom-call | flops 5284823040 | bytes 12000000 | tf_op jit(solution)/shard_map/pallas_call | solution.py:210
  126.5 4.9 %shard_map.71 = (bf16[80,4096]{1,0:T(8,128)(2,1)}, bf16[80,4096]{1,0:T(8,128)(2,1)}) custom-call(bf16[640,512]{1,0:T(8,128)(2,1)} %shard_map.69.hidden_ref, bf16[512,7168]{1,0:T(8,128)(2,1)} %bitcast.36), custom_call_target="tpu_custom_call" | custom-call | flops 671088640 | bytes 8000000 | tf_op jit(solution)/shard_map/pallas_call | solution.py:237
  131.4 6.6 %shard_map.72 = bf16[640,3072]{1,0:T(8,128)(2,1)} custom-call(bf16[320,320]{1,0:T(8,128)(2,1)} %get-tuple-element.40.unmix_ref, bf16[640,512]{1,0:T(8,128)(2,1)} %shard_map.69.hidden_ref, bf16[512,7168]{1,0:T(8,128)(2,1)} %bitcast.37), custom_call_target="tpu_custom_call" | custom-call | flops 2013265920 | bytes 8000000 | tf_op jit(solution)/shard_map/pallas_call | solution.py:261
  138.0 6.9 %all-to-all-start.3 = ((bf16[16,40,3072]{2,1,0:T(8,128)(2,1)}), bf16[16,40,3072]{2,1,0:T(8,128)(2,1)}, u32[]{:S(2)}, u32[]{:S(2)}) async-start(bf16[16,40,3072]{2,1,0:T(8,128)(2,1)} %bitcast.40), calls=%async_computation.3 | async-start | bytes 7864320 | tf_op jit(solution)/shard_map/all_to_all | solution.py:393
  144.9 6.0 %shard_map.70 = (bf16[160,4096]{1,0:T(8,128)(2,1)}, bf16[160,4096]{1,0:T(8,128)(2,1)}, bf16[160,4096]{1,0:T(8,128)(2,1)}) custom-call(bf16[640,512]{1,0:T(8,128)(2,1)} %shard_map.69.hidden_ref, bf16[512,7168]{1,0:T(8,128)(2,1)} %bitcast.38), custom_call_target="tpu_custom_call" | custom-call | flops 2013265920 | bytes 8000000 | tf_op jit(solution)/shard_map/pallas_call | solution.py:237
  152.3 3.3 %collective-permute-start.13 = (bf16[80,4096]{1,0:T(8,128)(2,1)S(1)}, bf16[80,4096]{1,0:T(8,128)(2,1)S(1)}, u32[]{:S(2)}, u32[]{:S(2)}) collective-permute-start(bf16[80,4096]{1,0:T(8,128)(2,1)S(1)} %copy-done.18), channel_id=1, source_target_pairs={{0,1},{1,2},{2,3},{3,0},{4,5},{5,6},{6,7},{7,4},{8,9},{9,10},{10,1... | collective-permute-start | bytes 1966088 | tf_op jit(solution)/shard_map/ppermute | solution.py:335
  156.9 10.4 %collective-permute-done.13 = bf16[80,4096]{1,0:T(8,128)(2,1)S(1)} collective-permute-done((bf16[80,4096]{1,0:T(8,128)(2,1)S(1)}, bf16[80,4096]{1,0:T(8,128)(2,1)S(1)}, u32[]{:S(2)}, u32[]{:S(2)}) %collective-permute-start.13) | collective-permute-done | bytes 655392 | tf_op jit(solution)/shard_map/ppermute | solution.py:335
  168.7 3.7 %collective-permute-start.14 = (bf16[160,4096]{1,0:T(8,128)(2,1)}, bf16[160,4096]{1,0:T(8,128)(2,1)}, u32[]{:S(2)}, u32[]{:S(2)}) collective-permute-start(bf16[160,4096]{1,0:T(8,128)(2,1)} %pad_maximum_fusion.1), channel_id=1, source_target_pairs={{0,1},{1,2},{2,3},{3,0},{4,5},{5,6},{6,7},{7,4},{8,9},{9,10},{10,1... | collective-permute-start | bytes 3932168 | tf_op jit(solution)/shard_map/ppermute | solution.py:335
  172.3 23.1 %all-to-all-done.3 = bf16[16,40,3072]{2,1,0:T(8,128)(2,1)} async-done(((bf16[16,40,3072]{2,1,0:T(8,128)(2,1)}), bf16[16,40,3072]{2,1,0:T(8,128)(2,1)}, u32[]{:S(2)}, u32[]{:S(2)}) %all-to-all-start.3) | async-done | bytes 3932192 | tf_op jit(solution)/shard_map/all_to_all | solution.py:393
  195.5 6.9 %shard_map.73 = (f32[256,3072]{1,0:T(8,128)}, bf16[256,3072]{1,0:T(8,128)(2,1)}) custom-call(bf16[640,3072]{1,0:T(8,128)(2,1)} %bitcast.16.rows_ref, bf16[64,3200]{1,0:T(8,128)(2,1)} %get-tuple-element.20.refs_0_.refs_8_, bf16[64,3200]{1,0:T(8,128)(2,1)} %copy-done.8, bf16[64,3200]{1,0:T(8,128)(2,1)} %copy-done.5, bf16[64,3200]{1,0:T(8,128)(2,1)} %copy-done.9, ...), custom_call_target="tpu_custom_call" | custom-call | flops 2013265920 | bytes 10000000 | tf_op jit(solution)/shard_map/pallas_call | solution.py:297
  202.4 2.3 add_convert_fusion
  204.8 4.2 %fusion.40 = bf16[1280,512]{1,0:T(8,128)(2,1)} fusion(bf16[1280,512]{1,0:T(8,128)(2,1)S(1)} %bitcast.48, s32[1280]{0:T(1024)S(1)} %get-tuple-element.47, s32[1280]{0:T(1024)S(1)} %get-tuple-element.48, s32[1280]{0:T(1024)S(1)} %get-tuple-element.50, s32[1280]{0:T(1024)S(1)} %get-tuple-element.52, s32[1280]{0:T(1024)S(1)} %get-tuple-element.54, ...), kind=kOutput, calls=%fused_computation.41 | convolution fusion | flops 1693122560 | bytes 2672640 | tf_op jit(solution)/shard_map/dot_general | solution.py:38
  209.1 4.3 %all-to-all-start.2 = ((bf16[32,40,512]{2,1,0:T(8,128)(2,1)}), bf16[32,40,512]{2,1,0:T(8,128)(2,1)S(1)}, u32[]{:S(2)}, u32[]{:S(2)}) async-start(bf16[32,40,512]{2,1,0:T(8,128)(2,1)} %bitcast.47), calls=%async_computation.2 | async-start | bytes 2621440 | tf_op jit(solution)/shard_map/all_to_all | solution.py:404
  213.4 2.5 %fusion.95 = (bf16[256,3072]{1,0:T(8,128)(2,1)S(1)}, f32[256,3072]{1,0:T(8,128)S(1)}) fusion(f32[256,3072]{1,0:T(8,128)} %get-tuple-element.33, bf16[256,3072]{1,0:T(8,128)(2,1)S(1)} %collective-permute-done.15), kind=kLoop, calls=%fused_computation.153 | loop fusion | flops 2359296 | bytes 9437184 | tf_op jit(solution)/shard_map/convert.2
  217.0 2.3 collective-permute-start.17
  221.4 11.8 %all-to-all-done.2 = bf16[32,40,512]{2,1,0:T(8,128)(2,1)S(1)} async-done(((bf16[32,40,512]{2,1,0:T(8,128)(2,1)}), bf16[32,40,512]{2,1,0:T(8,128)(2,1)S(1)}, u32[]{:S(2)}, u32[]{:S(2)}) %all-to-all-start.2) | async-done | bytes 1310752 | tf_op jit(solution)/shard_map/all_to_all | solution.py:404
  233.3 3.1 %collective-permute-done.17.b_ref = bf16[64,3072]{1,0:T(8,128)(2,1)S(1)} collective-permute-done((bf16[64,3072]{1,0:T(8,128)(2,1)S(1)}, bf16[64,3072]{1,0:T(8,128)(2,1)S(1)}, u32[]{:S(2)}, u32[]{:S(2)}) %collective-permute-start.17) | collective-permute-done | bytes 393248 | tf_op jit(solution)/shard_map/ppermute | solution.py:335
  238.3 4.3 %shard_map.74 = bf16[64,7168]{1,0:T(8,128)(2,1)} custom-call(bf16[1280,512]{1,0:T(8,128)(2,1)} %bitcast.42, s32[2,64]{1,0:T(2,128)} %bitcast.51, f32[2,64]{1,0:T(2,128)} %bitcast.53, f32[64,3072]{1,0:T(8,128)} %slice.49.kept, bf16[64,3072]{1,0:T(8,128)(2,1)} %copy-done.16, bf16[64,3072]{1,0:T(8,128)(2,1)} %copy-done.17, ...), custom_call_target="tpu_custom_call" | custom-call | flops 671088640 | bytes 5000000 | tf_op jit(solution)/shard_map/pallas_call | solution.py:326
  (88 shorter events, 19.4 us)
Async XLA Ops:
  3.8 7.6 %copy-start.4 = (bf16[64,3200]{1,0:T(8,128)(2,1)S(1)}, bf16[64,3200]{1,0:T(8,128)(2,1)}, u32[]{:S(2)}) copy-start(bf16[64,3200]{1,0:T(8,128)(2,1)} %get-tuple-element.20.refs_0_.refs_8_) | copy-start | bytes 1228804
  3.8 39.7 %all-to-all-start.1 = ((bf16[32,40,512]{2,1,0:T(8,128)(2,1)}), bf16[32,40,512]{2,1,0:T(8,128)(2,1)}, u32[]{:S(2)}, u32[]{:S(2)}) async-start(bf16[32,40,512]{2,1,0:T(8,128)(2,1)} %bitcast.46), calls=%async_computation.1 | async-start | bytes 2621440 | tf_op jit(solution)/shard_map/all_to_all | solution.py:354
  11.4 12.4 %collective-permute-start.1 = (bf16[64,3200]{1,0:T(8,128)(2,1)S(1)}, bf16[64,3200]{1,0:T(8,128)(2,1)S(1)}, u32[]{:S(2)}, u32[]{:S(2)}) collective-permute-start(bf16[64,3200]{1,0:T(8,128)(2,1)S(1)} %copy-done.4), channel_id=1, source_target_pairs={{0,1},{1,2},{2,3},{3,0},{4,5},{5,6},{6,7},{7,4},{8,9},{9,10},{10,1... | collective-permute-start | bytes 1228808 | tf_op jit(solution)/shard_map/ppermute | solution.py:335
  11.5 14.0 %collective-permute-start.3 = (bf16[64,3200]{1,0:T(8,128)(2,1)S(1)}, bf16[64,3200]{1,0:T(8,128)(2,1)S(1)}, u32[]{:S(2)}, u32[]{:S(2)}) collective-permute-start(bf16[64,3200]{1,0:T(8,128)(2,1)S(1)} %copy-done.4), channel_id=1, source_target_pairs={{0,2},{1,3},{2,0},{3,1},{4,6},{5,7},{6,4},{7,5},{8,10},{9,11},{10,... | collective-permute-start | bytes 1228808 | tf_op jit(solution)/shard_map/ppermute | solution.py:335
  14.0 19.5 %collective-permute-start.5 = (bf16[64,3200]{1,0:T(8,128)(2,1)S(1)}, bf16[64,3200]{1,0:T(8,128)(2,1)S(1)}, u32[]{:S(2)}, u32[]{:S(2)}) collective-permute-start(bf16[64,3200]{1,0:T(8,128)(2,1)S(1)} %copy-done.4), channel_id=1, source_target_pairs={{0,3},{1,0},{2,1},{3,2},{4,7},{5,4},{6,5},{7,6},{8,11},{9,8},{10,9... | collective-permute-start | bytes 1228808 | tf_op jit(solution)/shard_map/ppermute | solution.py:335
  14.0 19.5 %collective-permute-start = (bf16[64,3200]{1,0:T(8,128)(2,1)S(1)}, bf16[64,3200]{1,0:T(8,128)(2,1)S(1)}, u32[]{:S(2)}, u32[]{:S(2)}) collective-permute-start(bf16[64,3200]{1,0:T(8,128)(2,1)S(1)} %copy-done.4), channel_id=1, source_target_pairs={{0,16},{16,0},{1,17},{17,1},{2,18},{18,2},{3,19},{19,3},{4,20},{20... | collective-permute-start | bytes 1228808 | tf_op jit(solution)/shard_map/ppermute | solution.py:339
  23.8 11.4 %copy-start.5 = (bf16[64,3200]{1,0:T(8,128)(2,1)}, bf16[64,3200]{1,0:T(8,128)(2,1)S(1)}, u32[]{:S(2)}) copy-start(bf16[64,3200]{1,0:T(8,128)(2,1)S(1)} %collective-permute-done.1.refs_2_.refs_10_) | copy-start | bytes 1228804
  23.8 9.6 %collective-permute-start.2 = (bf16[64,3200]{1,0:T(8,128)(2,1)S(1)}, bf16[64,3200]{1,0:T(8,128)(2,1)S(1)}, u32[]{:S(2)}, u32[]{:S(2)}) collective-permute-start(bf16[64,3200]{1,0:T(8,128)(2,1)S(1)} %collective-permute-done.1.refs_2_.refs_10_), channel_id=1, source_target_pairs={{0,16},{16,0},{1,17},{17,1},{2,18},{18,2},{3,19},{19,3},{4,20},{20... | collective-permute-start | bytes 1228808 | tf_op jit(solution)/shard_map/ppermute | solution.py:339
  25.5 9.7 %copy-start.6 = (bf16[64,3200]{1,0:T(8,128)(2,1)}, bf16[64,3200]{1,0:T(8,128)(2,1)S(1)}, u32[]{:S(2)}) copy-start(bf16[64,3200]{1,0:T(8,128)(2,1)S(1)} %collective-permute-done.3.refs_4_.refs_12_) | copy-start | bytes 1228804
  25.5 8.0 %collective-permute-start.4 = (bf16[64,3200]{1,0:T(8,128)(2,1)S(1)}, bf16[64,3200]{1,0:T(8,128)(2,1)S(1)}, u32[]{:S(2)}, u32[]{:S(2)}) collective-permute-start(bf16[64,3200]{1,0:T(8,128)(2,1)S(1)} %collective-permute-done.3.refs_4_.refs_12_), channel_id=1, source_target_pairs={{0,16},{16,0},{1,17},{17,1},{2,18},{18,2},{3,19},{19,3},{4,20},{20... | collective-permute-start | bytes 1228808 | tf_op jit(solution)/shard_map/ppermute | solution.py:339
  33.4 1.7 collective-permute-start.6
  43.5 71.3 %all-to-all-start = ((bf16[16,40,3072]{2,1,0:T(8,128)(2,1)}), bf16[16,40,3072]{2,1,0:T(8,128)(2,1)}, u32[]{:S(2)}, u32[]{:S(2)}) async-start(bf16[16,40,3072]{2,1,0:T(8,128)(2,1)} %bitcast.39), calls=%async_computation | async-start | bytes 7864320 | tf_op jit(solution)/shard_map/all_to_all | solution.py:376
  55.2 39.1 %copy-start.1 = (bf16[20,8,8,512]{3,1,2,0:T(8,128)(2,1)}, bf16[20,8,8,512]{3,1,2,0:T(8,128)(2,1)S(1)}, u32[]{:S(2)}) copy-start(bf16[20,8,8,512]{3,1,2,0:T(8,128)(2,1)S(1)} %copy.11) | copy-start | bytes 3932164
  55.3 31.8 %collective-permute-start.8 = (bf16[160,4096]{1,0:T(8,128)(2,1)S(1)}, bf16[160,4096]{1,0:T(8,128)(2,1)S(1)}, u32[]{:S(2)}, u32[]{:S(2)}) collective-permute-start(bf16[160,4096]{1,0:T(8,128)(2,1)S(1)} %bitcast.43), channel_id=1, source_target_pairs={{0,3},{1,0},{2,1},{3,2},{4,7},{5,4},{6,5},{7,6},{8,11},{9,8},{10,9... | collective-permute-start | bytes 3932168 | tf_op jit(solution)/shard_map/ppermute | solution.py:335
  56.0 32.1 %collective-permute-start.7 = (bf16[160,4096]{1,0:T(8,128)(2,1)S(1)}, bf16[160,4096]{1,0:T(8,128)(2,1)S(1)}, u32[]{:S(2)}, u32[]{:S(2)}) collective-permute-start(bf16[160,4096]{1,0:T(8,128)(2,1)S(1)} %bitcast.44), channel_id=1, source_target_pairs={{0,1},{1,2},{2,3},{3,0},{4,5},{5,6},{6,7},{7,4},{8,9},{9,10},{10,1... | collective-permute-start | bytes 3932168 | tf_op jit(solution)/shard_map/ppermute | solution.py:335
  87.1 13.4 %copy-start.2 = (bf16[160,4096]{1,0:T(8,128)(2,1)}, bf16[160,4096]{1,0:T(8,128)(2,1)S(1)}, u32[]{:S(2)}) copy-start(bf16[160,4096]{1,0:T(8,128)(2,1)S(1)} %collective-permute-done.8.refs_1_) | copy-start | bytes 3932164
  88.0 19.7 %collective-permute-start.10 = (bf16[80,4096]{1,0:T(8,128)(2,1)}, bf16[80,4096]{1,0:T(8,128)(2,1)S(1)}, u32[]{:S(2)}, u32[]{:S(2)}) collective-permute-start(bf16[80,4096]{1,0:T(8,128)(2,1)} %slice.48), channel_id=1, source_target_pairs={{0,3},{1,0},{2,1},{3,2},{4,7},{5,4},{6,5},{7,6},{8,11},{9,8},{10,9... | collective-permute-start | bytes 1966088 | tf_op jit(solution)/shard_map/ppermute | solution.py:335
  90.0 17.8 %collective-permute-start.9 = (bf16[80,4096]{1,0:T(8,128)(2,1)}, bf16[80,4096]{1,0:T(8,128)(2,1)}, u32[]{:S(2)}, u32[]{:S(2)}) collective-permute-start(bf16[80,4096]{1,0:T(8,128)(2,1)} %slice.47), channel_id=1, source_target_pairs={{0,1},{1,2},{2,3},{3,0},{4,5},{5,6},{6,7},{7,4},{8,9},{9,10},{10,1... | collective-permute-start | bytes 1966088 | tf_op jit(solution)/shard_map/ppermute | solution.py:335
  131.4 24.2 %collective-permute-start.11 = (bf16[80,4096]{1,0:T(8,128)(2,1)}, bf16[80,4096]{1,0:T(8,128)(2,1)S(1)}, u32[]{:S(2)}, u32[]{:S(2)}) collective-permute-start(bf16[80,4096]{1,0:T(8,128)(2,1)} %get-tuple-element.30), channel_id=1, source_target_pairs={{0,3},{1,0},{2,1},{3,2},{4,7},{5,4},{6,5},{7,6},{8,11},{9,8},{10,9... | collective-permute-start | bytes 1966088 | tf_op jit(solution)/shard_map/ppermute | solution.py:335
  138.0 57.5 %all-to-all-start.3 = ((bf16[16,40,3072]{2,1,0:T(8,128)(2,1)}), bf16[16,40,3072]{2,1,0:T(8,128)(2,1)}, u32[]{:S(2)}, u32[]{:S(2)}) async-start(bf16[16,40,3072]{2,1,0:T(8,128)(2,1)} %bitcast.40), calls=%async_computation.3 | async-start | bytes 7864320 | tf_op jit(solution)/shard_map/all_to_all | solution.py:393
  144.9 7.3 %copy-start.18 = (bf16[80,4096]{1,0:T(8,128)(2,1)S(1)}, bf16[80,4096]{1,0:T(8,128)(2,1)}, u32[]{:S(2)}) copy-start(bf16[80,4096]{1,0:T(8,128)(2,1)} %get-tuple-element.32) | copy-start | bytes 1966084
  152.3 15.0 %collective-permute-start.13 = (bf16[80,4096]{1,0:T(8,128)(2,1)S(1)}, bf16[80,4096]{1,0:T(8,128)(2,1)S(1)}, u32[]{:S(2)}, u32[]{:S(2)}) collective-permute-start(bf16[80,4096]{1,0:T(8,128)(2,1)S(1)} %copy-done.18), channel_id=1, source_target_pairs={{0,1},{1,2},{2,3},{3,0},{4,5},{5,6},{6,7},{7,4},{8,9},{9,10},{10,1... | collective-permute-start | bytes 1966088 | tf_op jit(solution)/shard_map/ppermute | solution.py:335
  156.9 45.4 %collective-permute-start.12 = (bf16[160,4096]{1,0:T(8,128)(2,1)}, bf16[160,4096]{1,0:T(8,128)(2,1)}, u32[]{:S(2)}, u32[]{:S(2)}) collective-permute-start(bf16[160,4096]{1,0:T(8,128)(2,1)} %pad_maximum_fusion), channel_id=1, source_target_pairs={{0,3},{1,0},{2,1},{3,2},{4,7},{5,4},{6,5},{7,6},{8,11},{9,8},{10,9... | collective-permute-start | bytes 3932168 | tf_op jit(solution)/shard_map/ppermute | solution.py:335
  168.7 33.7 %collective-permute-start.14 = (bf16[160,4096]{1,0:T(8,128)(2,1)}, bf16[160,4096]{1,0:T(8,128)(2,1)}, u32[]{:S(2)}, u32[]{:S(2)}) collective-permute-start(bf16[160,4096]{1,0:T(8,128)(2,1)} %pad_maximum_fusion.1), channel_id=1, source_target_pairs={{0,1},{1,2},{2,3},{3,0},{4,5},{5,6},{6,7},{7,4},{8,9},{9,10},{10,1... | collective-permute-start | bytes 3932168 | tf_op jit(solution)/shard_map/ppermute | solution.py:335
  195.5 6.9 %copy-start.12 = (bf16[160,4096]{1,0:T(8,128)(2,1)S(1)}, bf16[160,4096]{1,0:T(8,128)(2,1)}, u32[]{:S(2)}) copy-start(bf16[160,4096]{1,0:T(8,128)(2,1)} %get-tuple-element.28) | copy-start | bytes 3932164
  202.3 11.1 %collective-permute-start.15 = (bf16[256,3072]{1,0:T(8,128)(2,1)}, bf16[256,3072]{1,0:T(8,128)(2,1)S(1)}, u32[]{:S(2)}, u32[]{:S(2)}) collective-permute-start(bf16[256,3072]{1,0:T(8,128)(2,1)} %get-tuple-element.34), channel_id=1, source_target_pairs={{0,16},{16,0},{1,17},{17,1},{2,18},{18,2},{3,19},{19,3},{4,20},{20... | collective-permute-start | bytes 4718600 | tf_op jit(solution)/shard_map/ppermute | solution.py:339
  209.1 24.2 %all-to-all-start.2 = ((bf16[32,40,512]{2,1,0:T(8,128)(2,1)}), bf16[32,40,512]{2,1,0:T(8,128)(2,1)S(1)}, u32[]{:S(2)}, u32[]{:S(2)}) async-start(bf16[32,40,512]{2,1,0:T(8,128)(2,1)} %bitcast.47), calls=%async_computation.2 | async-start | bytes 2621440 | tf_op jit(solution)/shard_map/all_to_all | solution.py:404
  216.1 17.2 %collective-permute-start.16 = (bf16[64,3072]{1,0:T(8,128)(2,1)S(1)}, bf16[64,3072]{1,0:T(8,128)(2,1)S(1)}, u32[]{:S(2)}, u32[]{:S(2)}) collective-permute-start(bf16[64,3072]{1,0:T(8,128)(2,1)S(1)} %get-tuple-element.39), channel_id=1, source_target_pairs={{0,3},{1,0},{2,1},{3,2},{4,7},{5,4},{6,5},{7,6},{8,11},{9,8},{10,9... | collective-permute-start | bytes 1179656 | tf_op jit(solution)/shard_map/ppermute | solution.py:335
  217.0 19.3 %collective-permute-start.17 = (bf16[64,3072]{1,0:T(8,128)(2,1)S(1)}, bf16[64,3072]{1,0:T(8,128)(2,1)S(1)}, u32[]{:S(2)}, u32[]{:S(2)}) collective-permute-start(bf16[64,3072]{1,0:T(8,128)(2,1)S(1)} %get-tuple-element.38), channel_id=1, source_target_pairs={{0,1},{1,2},{2,3},{3,0},{4,5},{5,6},{6,7},{7,4},{8,9},{9,10},{10,1... | collective-permute-start | bytes 1179656 | tf_op jit(solution)/shard_map/ppermute | solution.py:335
  219.4 18.9 %collective-permute-start.18 = (bf16[64,3072]{1,0:T(8,128)(2,1)S(1)}, bf16[64,3072]{1,0:T(8,128)(2,1)}, u32[]{:S(2)}, u32[]{:S(2)}) collective-permute-start(bf16[64,3072]{1,0:T(8,128)(2,1)S(1)} %get-tuple-element.37), channel_id=1, source_target_pairs={{0,2},{1,3},{2,0},{3,1},{4,6},{5,7},{6,4},{7,5},{8,10},{9,11},{10,... | collective-permute-start | bytes 1179656 | tf_op jit(solution)/shard_map/ppermute | solution.py:335
  233.3 5.0 %copy-start = (bf16[32,40,512]{2,1,0:T(8,128)(2,1)}, bf16[32,40,512]{2,1,0:T(8,128)(2,1)S(1)}, u32[]{:S(2)}) copy-start(bf16[32,40,512]{2,1,0:T(8,128)(2,1)S(1)} %all-to-all-done.2) | copy-start | bytes 3932164
  233.3 5.0 %copy-start.16 = (bf16[64,3072]{1,0:T(8,128)(2,1)}, bf16[64,3072]{1,0:T(8,128)(2,1)S(1)}, u32[]{:S(2)}) copy-start(bf16[64,3072]{1,0:T(8,128)(2,1)S(1)} %collective-permute-done.16.a_ref) | copy-start | bytes 1179652
  (10 other events, 20.9 us)
